TPU v7x, 256 devices: a whole 4x4x8 slice. The times are simulated.
256 devices in a mesh: section: 4 (over y), seq: 64 (over z, x, core).
Axes of the slice: x: 4, y: 4, z: 8, core: 2. Of those that a mesh axis runs over, the one named last changes fastest.
Arguments:
- patches: bfloat16 [64, 729, 1152], P('seq'), may hold values from -40 to 40
- fc_gain: float32 [4, 1152], P('section'), may hold values from 0.1 to 1.9
- fc_in: bfloat16 [4, 1152, 2176], P('section', 'seq'), may hold values from -0.1875 to 0.1875
- fc_in_bias: float32 [4, 2176], P('section'), may hold values from -3 to 3
- fc_out: bfloat16 [4, 2176, 1152], P('section', None, 'seq'), may hold values from -0.125 to 0.125
- fc_out_bias: float32 [4, 1152], P('section'), may hold values from -3 to 3
- proj_weight: bfloat16 [1152, 3584], P('seq'), may hold values from -0.1875 to 0.1875
- text_embed: bfloat16 [8192, 3584], P('seq'), may hold values from -40 to 40
- frame_start: int32 [64], replicated, may hold values from 0 to 8191, as said below
- frame_count: int32 [64], replicated, may hold values from 1 to 196, as said below
- segment_ids: int32 [8192], replicated, may hold values from 0 to 2, as said below
- norm_gain: float32 [3584], replicated, may hold values from 0.1 to 1.9
- query_weight: bfloat16 [3584, 2048], P(None, 'section'), may hold values from -3 to 3
- query_bias: float32 [2048], P('section'), may hold values from -3 to 3
- key_weight: bfloat16 [3584, 512], P(None, 'section'), may hold values from -1 to 1
- value_weight: bfloat16 [3584, 512], P(None, 'section'), may hold values from -0.09375 to 0.09375
- value_bias: float32 [512], P('section'), may hold values from -3 to 3
Outputs:
- attended: bfloat16 [8192, 2048], P('seq', 'section')
Inputs may be any that keep to these rules, and one draw needn't show every extreme that they name: Frame f keeps its first frame_count[f] pooled tokens and places them at positions frame_start[f] to frame_start[f] + frame_count[f] - 1; frame f begins in shard f, at a position from f * 128 to (f + 1) * 128 - 1; every frame ends before the next one begins, and the last ends by position 8191. The frame of shard 64 / 2 - 1 runs into the next shard. `frame_count`: some frame keeps all 196 tokens. `segment_ids`: segment numbers never fall along the sequence, and each of 0, 1 and 2 occurs.
All inputs are finite; a program needn't handle non-finite values.
Results may differ from a plain program's by a relative error of at most 0.02.
Values may be sent and summed in bfloat16 or wider, within the bound.
A program may use at most 128 MiB of HBM per device.

v0:
```python
import math

import jax
import jax.numpy as jnp
from jax import lax
from jax.sharding import PartitionSpec as P

GRID = 27


layer_eps = 1e-06
rms_eps = 1e-06
rope_base = 1000000.0
mask_floor = -1e30


def turned_gather(arrays, axis, dims):
    turned = [jnp.moveaxis(a, dim, 0) for a, dim in zip(arrays, dims)]
    both = jnp.concatenate([t.reshape(len(t), -1) for t in turned], axis=1)
    filled, at, finished = (lax.all_gather(both, axis, axis=0, tiled=True), 0, [])
    for t, dim in zip(turned, dims):
        section = filled[:, at : at + t[0].size].reshape(-1, *t.shape[1:])
        finished.append(jnp.moveaxis(section, 0, dim))
        at += t[0].size
    return tuple(finished)


def passed_along(block, axis, distance):
    devices = range(lax.axis_size(axis))
    route = [(i - distance, i) for i in devices if i - distance in devices]
    return lax.ppermute(block, axis, route)


def from_root(x, axis, root):
    return lax.dynamic_index_in_dim(lax.all_gather(x, axis), root, 0, keepdims=False)


def layer_norm(values, scales):
    widened = values.astype(jnp.float32)
    center = widened - jnp.mean(widened, axis=-1, keepdims=True)
    spread = jnp.mean(center * center, axis=-1, keepdims=True)
    return center * lax.rsqrt(spread + layer_eps) * scales


def encoder_layer(values, scales, w_in, b_in, w_out, b_out):
    normed = layer_norm(values, scales).astype(jnp.bfloat16)
    hidden = jax.nn.gelu(
        jnp.dot(normed, w_in, preferred_element_type=jnp.float32) + b_in, approximate=True
    ).astype(jnp.bfloat16)
    summed = (
        values.astype(jnp.float32)
        + jnp.dot(hidden, w_out, preferred_element_type=jnp.float32)
        + b_out
    )
    return summed.astype(jnp.bfloat16)


def pool_frame(encoded):
    channel = encoded.shape[-1]
    grid_side = GRID
    pool_side = (GRID + 1) // 2
    grid_cells = encoded.astype(jnp.float32).reshape(grid_side, grid_side, channel)
    pad_cells = 2 * pool_side - grid_side
    grid_cells = jnp.pad(grid_cells, [(0, pad_cells), (0, pad_cells), (0, 0)])
    totals = grid_cells.reshape(pool_side, 2, pool_side, 2, channel).sum(axis=(1, 3))
    counts = jnp.minimum(2, grid_side - 2 * jnp.arange(pool_side)).astype(jnp.float32)
    cell_area = counts[:, None] * counts[None, :]
    return (totals / cell_area[..., None]).reshape(pool_side * pool_side, channel)


def rotate(values, positions):
    head_dim = values.shape[-1]
    half_dim = head_dim // 2
    inv_rates = jnp.exp(
        jnp.arange(half_dim, dtype=jnp.float32) * (-2.0 * math.log(rope_base) / head_dim)
    )
    angles = positions.astype(jnp.float32)[:, None] * inv_rates[None, :]
    cosine = jnp.cos(angles)[:, None, :]
    sine_part = jnp.sin(angles)[:, None, :]
    first_half = values[..., :half_dim]
    second = values[..., half_dim:]
    return jnp.concatenate(
        [first_half * cosine - second * sine_part, second * cosine + first_half * sine_part],
        axis=-1,
    )


def take_rows(source, offsets, upper_limit):
    is_valid = (offsets >= 0) & (offsets < upper_limit)
    picked = jnp.take(source, jnp.clip(offsets, 0, source.shape[0] - 1), axis=0)
    return (jnp.where(is_valid[:, None], picked, jnp.zeros((), source.dtype)), is_valid)


def attend_block(softmax_state, queries, query_pos, query_seg, key_block, block_start, segment_ids):
    row_top, row_total, row_acc = softmax_state
    head_dim = queries.shape[1]
    key_part = key_block[:, :head_dim]
    value_part = key_block[:, head_dim:]
    scores = lax.dot_general(
        queries, key_part, (((1,), (1,)), ((), ())), preferred_element_type=jnp.float32
    )
    scores = scores * (1.0 / math.sqrt(head_dim))
    key_pos = block_start + jnp.arange(key_block.shape[0], dtype=jnp.int32)
    key_seg = lax.dynamic_slice_in_dim(segment_ids, block_start, key_block.shape[0], 0)
    allowed = (key_pos[None, :] <= query_pos[:, None]) & (key_seg[None, :] == query_seg[:, None])
    masked = jnp.where(allowed, scores, mask_floor)
    new_top = jnp.maximum(row_top, jnp.max(masked, axis=1))
    weights = jnp.where(allowed, jnp.exp(masked - new_top[:, None]), 0.0)
    keep_old = jnp.exp(row_top - new_top)
    row_total = row_total * keep_old + jnp.sum(weights, axis=1)
    row_acc = row_acc * keep_old[:, None] + jnp.dot(
        weights.astype(jnp.bfloat16), value_part, preferred_element_type=jnp.float32
    )
    return (new_top, row_total, row_acc)


def per_device(
    patches,
    fc_gain,
    fc_in,
    fc_in_bias,
    fc_out,
    fc_out_bias,
    proj_weight,
    text_embed,
    frame_start,
    frame_count,
    segment_ids,
    norm_gain,
    query_weight,
    query_bias,
    key_weight,
    value_weight,
    value_bias,
):
    section_count = lax.axis_size("section")
    section_id = lax.axis_index("section")
    shard_count = lax.axis_size("seq")
    shard_id = lax.axis_index("seq")
    shard_rows = text_embed.shape[0]
    model_width = text_embed.shape[1]
    head_size = key_weight.shape[1]
    group_size = query_weight.shape[1] // head_size
    frame_patches = patches[0]
    patch_rows, feature_width = frame_patches.shape
    column_count = model_width // section_count
    proj_block = lax.dynamic_slice_in_dim(proj_weight, section_id * column_count, column_count, 1)
    w_in, w_out, proj_full = turned_gather((fc_in, fc_out, proj_block), "seq", (1, 2, 0))
    w_in = w_in[0]
    w_out = w_out[0]
    layer_gain = fc_gain[0]
    bias_in = fc_in_bias[0]
    bias_out = fc_out_bias[0]
    band_rows = 9
    batch_rows = band_rows * GRID
    batches = GRID // band_rows
    tick_count = batches + section_count - 1
    first_section = section_id == 0
    last_section = section_id == section_count - 1

    def run_tick(tick_index, loop_carry):
        inflow, collected = loop_carry
        feed_rows = lax.dynamic_slice_in_dim(
            frame_patches, jnp.minimum(tick_index, batches - 1) * batch_rows, batch_rows, 0
        )
        result = encoder_layer(
            jnp.where(first_section, feed_rows, inflow), layer_gain, w_in, bias_in, w_out, bias_out
        )
        slot_start = jnp.clip(tick_index - section_count + 1, 0, batches - 1) * batch_rows
        current = lax.dynamic_slice_in_dim(collected, slot_start, batch_rows, 0)
        is_ready = last_section & (tick_index >= section_count - 1)
        collected = lax.dynamic_update_slice_in_dim(
            collected, jnp.where(is_ready, result, current), slot_start, 0
        )
        inflow = passed_along(result, "section", 1)
        return (inflow, collected)

    start_state = (
        jnp.zeros((batch_rows, feature_width), jnp.bfloat16),
        jnp.zeros((patch_rows, feature_width), jnp.bfloat16),
    )
    inflow, collected = lax.fori_loop(0, tick_count, run_tick, start_state)
    pooled = pool_frame(collected).astype(jnp.bfloat16)
    local_slots = jnp.arange(shard_rows, dtype=jnp.int32)
    positions = shard_id * shard_rows + local_slots
    own_start = frame_start[shard_id]
    own_count = frame_count[shard_id]
    previous = jnp.maximum(shard_id - 1, 0)
    prev_offsets = positions - frame_start[previous]
    prev_valid = (shard_id > 0) & (prev_offsets >= 0) & (prev_offsets < frame_count[previous])
    own_rows, own_valid = take_rows(pooled, positions - own_start, own_count)
    sent_rows, sent_valid = take_rows(pooled, positions + shard_rows - own_start, own_count)
    arrived = passed_along(sent_rows, "seq", 1)
    vision = jnp.where(own_valid[:, None], own_rows, arrived)
    vision = from_root(vision, "section", section_count - 1)
    block_cols = jnp.dot(vision, proj_full, preferred_element_type=jnp.float32).astype(jnp.bfloat16)
    text_cols = lax.dynamic_slice_in_dim(text_embed, section_id * column_count, column_count, 1)
    mixed_cols = jnp.where((own_valid | prev_valid)[:, None], block_cols, text_cols)
    inputs = lax.all_gather(mixed_cols, "section", axis=1, tiled=True)
    widened = inputs.astype(jnp.float32)
    normed = (
        widened
        * lax.rsqrt(jnp.mean(widened * widened, axis=1, keepdims=True) + rms_eps)
        * norm_gain
    ).astype(jnp.bfloat16)
    queries = jnp.dot(normed, query_weight, preferred_element_type=jnp.float32) + query_bias
    queries = rotate(queries.reshape(shard_rows, group_size, head_size), positions).astype(
        jnp.bfloat16
    )
    queries = queries.reshape(shard_rows * group_size, head_size)
    key_heads = jnp.dot(normed, key_weight, preferred_element_type=jnp.float32)
    key_heads = rotate(key_heads.reshape(shard_rows, 1, head_size), positions).astype(jnp.bfloat16)
    key_heads = key_heads.reshape(shard_rows, head_size)
    values = (
        jnp.dot(normed, value_weight, preferred_element_type=jnp.float32) + value_bias
    ).astype(jnp.bfloat16)
    stacked = jnp.concatenate([key_heads, values], axis=1)
    query_pos = jnp.repeat(positions, group_size)
    query_seg = jnp.repeat(
        lax.dynamic_slice_in_dim(segment_ids, shard_id * shard_rows, shard_rows, 0), group_size
    )
    query_total = shard_rows * group_size
    blank_state = (
        jnp.full((query_total,), mask_floor, jnp.float32),
        jnp.zeros((query_total,), jnp.float32),
        jnp.zeros((query_total, head_size), jnp.float32),
    )
    half_count = shard_count // 2
    is_lower = shard_id < half_count
    quarter = shard_count // 4
    partner_queries = passed_along(queries, "seq", -half_count)
    partner_id = shard_id + half_count
    partner_pos = jnp.repeat(partner_id * shard_rows + local_slots, group_size)
    partner_seg = jnp.repeat(
        lax.dynamic_slice_in_dim(
            segment_ids, jnp.minimum(partner_id, shard_count - 1) * shard_rows, shard_rows, 0
        ),
        group_size,
    )
    own_low = jnp.where(is_lower, 0, quarter * shard_rows)
    own_high = (shard_id + 1) * shard_rows
    part_high = jnp.where(is_lower, quarter * shard_rows, 0)

    def visit_pair(pair_state, key_block, block_start):
        own_state, other_state = pair_state
        own_state = lax.cond(
            (block_start >= own_low) & (block_start < own_high),
            lambda carried: attend_block(
                carried, queries, query_pos, query_seg, key_block, block_start, segment_ids
            ),
            lambda carried: carried,
            own_state,
        )
        other_state = lax.cond(
            block_start < part_high,
            lambda carried: attend_block(
                carried,
                partner_queries,
                partner_pos,
                partner_seg,
                key_block,
                block_start,
                segment_ids,
            ),
            lambda carried: carried,
            other_state,
        )
        return (own_state, other_state)

    initial = (blank_state, blank_state)
    arrived_rows = lax.all_gather(stacked, "seq", axis=0, tiled=True)
    sub_rows = math.gcd(arrived_rows.shape[0], shard_rows)

    def visit_one(block_index, inner_state):
        key_block = lax.dynamic_slice_in_dim(arrived_rows, block_index * sub_rows, sub_rows, 0)
        return visit_pair(inner_state, key_block, block_index * sub_rows)

    folded = lax.fori_loop(0, arrived_rows.shape[0] // sub_rows, visit_one, initial)
    own_state, other_state = folded
    back_top, back_total, back_acc = passed_along(
        (other_state[0], other_state[1], other_state[2]), "seq", half_count
    )
    back_top = jnp.where(is_lower, mask_floor, back_top)
    back_total = jnp.where(is_lower, 0.0, back_total)
    back_acc = jnp.where(is_lower, 0.0, back_acc)
    own_top, own_total, own_acc = own_state
    row_top = jnp.maximum(own_top, back_top)
    keep_own = jnp.exp(own_top - row_top)
    keep_back = jnp.exp(back_top - row_top)
    row_total = own_total * keep_own + back_total * keep_back
    row_acc = own_acc * keep_own[:, None] + back_acc * keep_back[:, None]
    attended = (row_acc / row_total[:, None]).astype(jnp.bfloat16)
    return attended.reshape(shard_rows, group_size * head_size)


def solution(mesh):
    return jax.shard_map(
        per_device,
        mesh=mesh,
        in_specs=(
            P("seq", None, None),
            P("section", None),
            P("section", "seq", None),
            P("section", None),
            P("section", None, "seq"),
            P("section", None),
            P("seq", None),
            P("seq", None),
            P(),
            P(),
            P(),
            P(),
            P(None, "section"),
            P("section"),
            P(None, "section"),
            P(None, "section"),
            P("section"),
        ),
        out_specs=P("seq", "section"),
        check_vma=False,
    )
```

profile of v0, /device:TPU:231, one launch (start us, length us, event | category | flops | bytes accessed | tf_op | source)
XLA Modules:
  0.0 614.5 jit_solution(5960631140011287223)
XLA Ops:
  13.4 91.2 %all-gather.10.cloned.1.call-done = bf16[64,18,5248]{2,1,0:T(8,128)(2,1)} async-done(((bf16[1,18,5248]{2,1,0:T(8,128)(2,1)}), bf16[64,18,5248]{2,1,0:T(8,128)(2,1)}) %all-gather.10.cloned.1.call-update) | async-done | bytes 12091408 | tf_op jit(solution)/shard_map/all_gather | solution.py:20
  104.6 17.1 %reshape.296 = bf16[1152,5248]{1,0:T(8,128)(2,1)} reshape(bf16[64,18,5248]{2,1,0:T(8,128)(2,1)} %all-gather.10.cloned.1.call-done) | data formatting | bytes 24182784
  121.7 8.4 %slice_bitcast_fusion = (bf16[2176,1152]{0,1:T(8,128)(2,1)}, bf16[1152,2176]{1,0:T(8,128)(2,1)}) fusion(bf16[1152,5248]{1,0:T(8,128)(2,1)} %reshape.296), kind=kLoop, calls=%fused_computation.76 | loop fusion | bytes 20054016 | tf_op jit(solution)/shard_map/squeeze | solution.py:150
  130.1 8.5 %copy.23 = bf16[2176,1152]{1,0:T(8,128)(2,1)} copy(bf16[2176,1152]{0,1:T(8,128)(2,1)} %get-tuple-element.956) | data formatting | bytes 10027008 | tf_op jit(solution)/shard_map/while | solution.py:182
  140.0 138.9 %while.43 = (s32[]{:T(128)}, bf16[243,1152]{1,0:T(8,128)(2,1)S(1)}, bf16[729,1152]{1,0:T(8,128)(2,1)}, pred[]{:T(512)}, bf16[729,1152]{1,0:T(8,128)(2,1)}, /*ind...) while((s32[]{:T(128)}, bf16[243,1152]{1,0:T(8,128)(2,1)S(1)}, ...), condition=%wide.region_3.4_spmd, body=%wide.region_0.3_spmd.sunk | while | flops 2446610432 | bytes 18521884 | solution.py:182
  141.8 7.5 %dynamic-slice_select_fusion.4 = (bf16[243,1152]{1,0:T(8,128)(2,1)S(1)}, bf16[243,1152]{1,0:T(8,128)(2,1)S(1)}) fusion(bf16[729,1152]{1,0:T(8,128)(2,1)} %get-tuple-element.1202, s32[]{:T(128)S(6)} %select_n.249, pred[]{:T(512)S(6)} %and.105, f32[1152]{0:T(1024)S(1)} %reduce.8, bf16[2176,1152]{1,0:T(8,128)(2,1)} %get-tuple-element.1227, ...), kind=kOutput, calls=%fused_computation.65.clone.1 | convolution fusion | flops 2444650496 | bytes 12880133 | tf_op jit(solution)/shard_map/while/body/eval_jaxpr/dot_general | solution.py:52
  149.4 3.1 collective-permute-start
  152.5 3.4 dynamic_update_slice.14
  156.0 8.5 %collective-permute-done = bf16[243,1152]{1,0:T(8,128)(2,1)S(1)} collective-permute-done((bf16[243,1152]{1,0:T(8,128)(2,1)S(1)}, bf16[243,1152]{1,0:T(8,128)(2,1)S(1)}, u32[]{:S(2)}, u32[]{:S(2)}) %collective-permute-start) | collective-permute-done | bytes 559904 | tf_op jit(solution)/shard_map/while/body/eval_jaxpr/ppermute | solution.py:31
  166.3 7.5 %dynamic-slice_select_fusion.4 = (bf16[243,1152]{1,0:T(8,128)(2,1)S(1)}, bf16[243,1152]{1,0:T(8,128)(2,1)S(1)}) fusion(bf16[729,1152]{1,0:T(8,128)(2,1)} %get-tuple-element.1202, s32[]{:T(128)S(6)} %select_n.249, pred[]{:T(512)S(6)} %and.105, f32[1152]{0:T(1024)S(1)} %reduce.8, bf16[2176,1152]{1,0:T(8,128)(2,1)} %get-tuple-element.1227, ...), kind=kOutput, calls=%fused_computation.65.clone.1 | convolution fusion | flops 2444650496 | bytes 12880133 | tf_op jit(solution)/shard_map/while/body/eval_jaxpr/dot_general | solution.py:52
  173.8 4.1 collective-permute-start
  178.0 3.4 dynamic_update_slice.14
  181.4 7.7 %collective-permute-done = bf16[243,1152]{1,0:T(8,128)(2,1)S(1)} collective-permute-done((bf16[243,1152]{1,0:T(8,128)(2,1)S(1)}, bf16[243,1152]{1,0:T(8,128)(2,1)S(1)}, u32[]{:S(2)}, u32[]{:S(2)}) %collective-permute-start) | collective-permute-done | bytes 559904 | tf_op jit(solution)/shard_map/while/body/eval_jaxpr/ppermute | solution.py:31
  190.9 7.5 %dynamic-slice_select_fusion.4 = (bf16[243,1152]{1,0:T(8,128)(2,1)S(1)}, bf16[243,1152]{1,0:T(8,128)(2,1)S(1)}) fusion(bf16[729,1152]{1,0:T(8,128)(2,1)} %get-tuple-element.1202, s32[]{:T(128)S(6)} %select_n.249, pred[]{:T(512)S(6)} %and.105, f32[1152]{0:T(1024)S(1)} %reduce.8, bf16[2176,1152]{1,0:T(8,128)(2,1)} %get-tuple-element.1227, ...), kind=kOutput, calls=%fused_computation.65.clone.1 | convolution fusion | flops 2444650496 | bytes 12880133 | tf_op jit(solution)/shard_map/while/body/eval_jaxpr/dot_general | solution.py:52
  198.4 4.1 collective-permute-start
  202.6 3.4 dynamic_update_slice.14
  206.0 6.8 %collective-permute-done = bf16[243,1152]{1,0:T(8,128)(2,1)S(1)} collective-permute-done((bf16[243,1152]{1,0:T(8,128)(2,1)S(1)}, bf16[243,1152]{1,0:T(8,128)(2,1)S(1)}, u32[]{:S(2)}, u32[]{:S(2)}) %collective-permute-start) | collective-permute-done | bytes 559904 | tf_op jit(solution)/shard_map/while/body/eval_jaxpr/ppermute | solution.py:31
  214.6 7.5 %dynamic-slice_select_fusion.4 = (bf16[243,1152]{1,0:T(8,128)(2,1)S(1)}, bf16[243,1152]{1,0:T(8,128)(2,1)S(1)}) fusion(bf16[729,1152]{1,0:T(8,128)(2,1)} %get-tuple-element.1202, s32[]{:T(128)S(6)} %select_n.249, pred[]{:T(512)S(6)} %and.105, f32[1152]{0:T(1024)S(1)} %reduce.8, bf16[2176,1152]{1,0:T(8,128)(2,1)} %get-tuple-element.1227, ...), kind=kOutput, calls=%fused_computation.65.clone.1 | convolution fusion | flops 2444650496 | bytes 12880133 | tf_op jit(solution)/shard_map/while/body/eval_jaxpr/dot_general | solution.py:52
  222.2 4.1 collective-permute-start
  226.3 3.4 dynamic_update_slice.14
  229.8 6.0 collective-permute-done
  237.5 7.5 %dynamic-slice_select_fusion.4 = (bf16[243,1152]{1,0:T(8,128)(2,1)S(1)}, bf16[243,1152]{1,0:T(8,128)(2,1)S(1)}) fusion(bf16[729,1152]{1,0:T(8,128)(2,1)} %get-tuple-element.1202, s32[]{:T(128)S(6)} %select_n.249, pred[]{:T(512)S(6)} %and.105, f32[1152]{0:T(1024)S(1)} %reduce.8, bf16[2176,1152]{1,0:T(8,128)(2,1)} %get-tuple-element.1227, ...), kind=kOutput, calls=%fused_computation.65.clone.1 | convolution fusion | flops 2444650496 | bytes 12880133 | tf_op jit(solution)/shard_map/while/body/eval_jaxpr/dot_general | solution.py:52
  245.1 4.1 collective-permute-start
  249.2 3.4 dynamic_update_slice.14
  252.7 5.1 collective-permute-done
  259.6 7.5 %dynamic-slice_select_fusion.4 = (bf16[243,1152]{1,0:T(8,128)(2,1)S(1)}, bf16[243,1152]{1,0:T(8,128)(2,1)S(1)}) fusion(bf16[729,1152]{1,0:T(8,128)(2,1)} %get-tuple-element.1202, s32[]{:T(128)S(6)} %select_n.249, pred[]{:T(512)S(6)} %and.105, f32[1152]{0:T(1024)S(1)} %reduce.8, bf16[2176,1152]{1,0:T(8,128)(2,1)} %get-tuple-element.1227, ...), kind=kOutput, calls=%fused_computation.65.clone.1 | convolution fusion | flops 2444650496 | bytes 12880133 | tf_op jit(solution)/shard_map/while/body/eval_jaxpr/dot_general | solution.py:52
  267.1 4.1 collective-permute-start
  271.2 3.4 dynamic_update_slice.14
  274.7 4.2 collective-permute-done
  278.9 2.5 reshape.266
  281.4 2.4 pad_convert_fusion
  283.8 5.5 reshape.273
  289.3 4.5 reduce_sum.76
  297.1 2.5 and_or_fusion
  300.5 3.0 collective-permute-done.1
  304.7 33.4 %all-gather.8.cloned.1.call-done = bf16[512,1152]{1,0:T(8,128)(2,1)} async-done(((bf16[128,1152]{1,0:T(8,128)(2,1)}), bf16[512,1152]{1,0:T(8,128)(2,1)}) %all-gather.8.cloned.1.call-update) | async-done | bytes 1179664 | tf_op jit(solution)/shard_map/all_gather | solution.py:35
  338.1 2.2 fusion.69
  340.3 12.5 %all_gather.18 = bf16[128,3584]{1,0:T(8,128)(2,1)S(1)} all-gather(bf16[128,896]{1,0:T(8,128)(2,1)S(1)} %fusion.69), channel_id=1, replica_groups=mesh['section'=4,'seq'=64] {'section'}, dimensions={1}, use_global_device_ids=true | all-gather | bytes 1146880 | tf_op jit(solution)/shard_map/all_gather | solution.py:199
  355.5 2.7 convolution_add_fusion.4
  358.7 4.5 collective-permute-start.2
  365.2 70.4 %all-gather.6.cloned.1.call-done = bf16[8192,256]{0,1:T(8,128)(2,1)} async-done(((bf16[128,256]{0,1:T(8,128)(2,1)}), bf16[8192,256]{0,1:T(8,128)(2,1)}) %all-gather.6.cloned.1.call-update) | async-done | bytes 4194320 | tf_op jit(solution)/shard_map/all_gather | solution.py:271
  435.7 158.5 %while.44 = (s32[]{:T(128)}, f32[512]{0:T(512)S(1)}, f32[512]{0:T(512)S(1)}, f32[512,128]{1,0:T(8,128)S(1)}, f32[512]{0:T(512)S(1)}, /*index=5*/f32[512]{0:T(512...) while((s32[]{:T(128)}, f32[512]{0:T(512)S(1)}, ...), condition=%wide.region_15.17_spmd.clone, body=%wide.region_6.16_spmd.clone.sunk | while | flops 69732624 | bytes 3403379 | solution.py:278
  453.6 1.9 conditional.6
  459.5 1.9 conditional.6
  465.4 1.9 conditional.6
  471.3 1.9 conditional.6
  477.2 1.9 conditional.6
  483.1 1.9 conditional.6
  489.0 1.9 conditional.6
  494.9 1.9 conditional.6
  500.8 1.9 conditional.6
  506.7 1.9 conditional.6
  512.6 1.9 conditional.6
  518.5 1.9 conditional.6
  524.4 1.9 conditional.6
  530.3 1.9 conditional.6
  536.2 1.9 conditional.6
  548.0 1.9 conditional.6
  553.9 1.9 conditional.6
  559.8 1.9 conditional.6
  565.7 1.9 conditional.6
  571.6 1.9 conditional.6
  577.5 1.9 conditional.6
  598.1 8.8 %collective-permute-done.3 = f32[512]{0:T(512)S(1)} collective-permute-done((f32[512]{0:T(512)S(1)}, f32[512]{0:T(512)S(1)}, u32[]{:S(2)}, u32[]{:S(2)}) %collective-permute-start.3) | collective-permute-done | bytes 2080 | tf_op jit(solution)/shard_map/ppermute | solution.py:31
  (927 shorter events, 237.2 us)
Async XLA Ops:
  6.5 346.5 %copy-start = (bf16[3584,128]{1,0:T(8,128)(2,1)S(1)}, bf16[3584,128]{1,0:T(8,128)(2,1)}, u32[]{:S(2)}) copy-start(bf16[3584,128]{1,0:T(8,128)(2,1)} %param.41) | copy-start | bytes 2752516
  6.5 98.1 %all-gather.10.cloned.1.call-start = ((), (), s32[]{:S(2)}) async-start(), calls=%async_computation.2 | async-start | bytes 16373760 | tf_op jit(solution)/shard_map/all_gather | solution.py:20
  9.1 329.0 %all-gather.8.cloned.1.call-start = ((), (), s32[]{:S(2)}) async-start(), calls=%async_computation.1 | async-start | bytes 1474560 | tf_op jit(solution)/shard_map/all_gather | solution.py:35
  138.6 1.4 copy-start.1
  138.6 1.4 copy-start.2
  138.6 1.4 copy-start.3
  149.4 15.1 %collective-permute-start = (bf16[243,1152]{1,0:T(8,128)(2,1)S(1)}, bf16[243,1152]{1,0:T(8,128)(2,1)S(1)}, u32[]{:S(2)}, u32[]{:S(2)}) collective-permute-start(bf16[243,1152]{1,0:T(8,128)(2,1)S(1)} %get-tuple-element.1143), channel_id=1, source_target_pairs={{0,64},{64,128},{128,192},{1,65},{65,129},{129,193},{2,66},{66,130... | collective-permute-start | bytes 1679624 | tf_op jit(solution)/shard_map/while/body/eval_jaxpr/ppermute | solution.py:31
  173.8 15.3 %collective-permute-start = (bf16[243,1152]{1,0:T(8,128)(2,1)S(1)}, bf16[243,1152]{1,0:T(8,128)(2,1)S(1)}, u32[]{:S(2)}, u32[]{:S(2)}) collective-permute-start(bf16[243,1152]{1,0:T(8,128)(2,1)S(1)} %get-tuple-element.1143), channel_id=1, source_target_pairs={{0,64},{64,128},{128,192},{1,65},{65,129},{129,193},{2,66},{66,130... | collective-permute-start | bytes 1679624 | tf_op jit(solution)/shard_map/while/body/eval_jaxpr/ppermute | solution.py:31
  198.4 14.4 %collective-permute-start = (bf16[243,1152]{1,0:T(8,128)(2,1)S(1)}, bf16[243,1152]{1,0:T(8,128)(2,1)S(1)}, u32[]{:S(2)}, u32[]{:S(2)}) collective-permute-start(bf16[243,1152]{1,0:T(8,128)(2,1)S(1)} %get-tuple-element.1143), channel_id=1, source_target_pairs={{0,64},{64,128},{128,192},{1,65},{65,129},{129,193},{2,66},{66,130... | collective-permute-start | bytes 1679624 | tf_op jit(solution)/shard_map/while/body/eval_jaxpr/ppermute | solution.py:31
  222.2 13.5 %collective-permute-start = (bf16[243,1152]{1,0:T(8,128)(2,1)S(1)}, bf16[243,1152]{1,0:T(8,128)(2,1)S(1)}, u32[]{:S(2)}, u32[]{:S(2)}) collective-permute-start(bf16[243,1152]{1,0:T(8,128)(2,1)S(1)} %get-tuple-element.1143), channel_id=1, source_target_pairs={{0,64},{64,128},{128,192},{1,65},{65,129},{129,193},{2,66},{66,130... | collective-permute-start | bytes 1679624 | tf_op jit(solution)/shard_map/while/body/eval_jaxpr/ppermute | solution.py:31
  245.1 12.7 %collective-permute-start = (bf16[243,1152]{1,0:T(8,128)(2,1)S(1)}, bf16[243,1152]{1,0:T(8,128)(2,1)S(1)}, u32[]{:S(2)}, u32[]{:S(2)}) collective-permute-start(bf16[243,1152]{1,0:T(8,128)(2,1)S(1)} %get-tuple-element.1143), channel_id=1, source_target_pairs={{0,64},{64,128},{128,192},{1,65},{65,129},{129,193},{2,66},{66,130... | collective-permute-start | bytes 1679624 | tf_op jit(solution)/shard_map/while/body/eval_jaxpr/ppermute | solution.py:31
  267.1 11.8 %collective-permute-start = (bf16[243,1152]{1,0:T(8,128)(2,1)S(1)}, bf16[243,1152]{1,0:T(8,128)(2,1)S(1)}, u32[]{:S(2)}, u32[]{:S(2)}) collective-permute-start(bf16[243,1152]{1,0:T(8,128)(2,1)S(1)} %get-tuple-element.1143), channel_id=1, source_target_pairs={{0,64},{64,128},{128,192},{1,65},{65,129},{129,193},{2,66},{66,130... | collective-permute-start | bytes 1679624 | tf_op jit(solution)/shard_map/while/body/eval_jaxpr/ppermute | solution.py:31
  295.1 8.4 %collective-permute-start.1 = (bf16[128,1152]{1,0:T(8,128)(2,1)S(1)}, bf16[128,1152]{1,0:T(8,128)(2,1)S(1)}, u32[]{:S(2)}, u32[]{:S(2)}) collective-permute-start(bf16[128,1152]{1,0:T(8,128)(2,1)S(1)} %select_select_fusion), channel_id=1, source_target_pairs={{0,1},{1,2},{2,3},{3,4},{4,5},{5,6},{6,7},{7,8},{8,9},{9,10},{10,1... | collective-permute-start | bytes 884744 | tf_op jit(solution)/shard_map/ppermute | solution.py:31
  304.4 131.2 %all-gather.6.cloned.1.call-start = ((), (), s32[]{:S(2)}) async-start(), calls=%async_computation | async-start | bytes 4259840 | tf_op jit(solution)/shard_map/all_gather | solution.py:271
  338.1 15.0 %copy-start.5 = (f32[3584]{0:T(1024)S(1)}, f32[3584]{0:T(1024)}, u32[]{:S(2)}) copy-start(f32[3584]{0:T(1024)} %param.38) | copy-start | bytes 43012
  340.2 13.4 %copy-start.4 = (bf16[3584,128]{1,0:T(8,128)(2,1)S(1)}, bf16[3584,128]{1,0:T(8,128)(2,1)}, u32[]{:S(2)}) copy-start(bf16[3584,128]{1,0:T(8,128)(2,1)} %param.42) | copy-start | bytes 2752516
  340.3 13.4 %copy-start.7 = (f32[128]{0:T(128)S(1)}, f32[128]{0:T(128)}, u32[]{:S(2)}) copy-start(f32[128]{0:T(128)} %param.43) | copy-start | bytes 1540
  353.1 2.4 copy-start.6
  358.7 6.5 %collective-permute-start.2 = (bf16[512,128]{1,0:T(8,128)(2,1)S(1)}, bf16[512,128]{1,0:T(8,128)(2,1)S(1)}, u32[]{:S(2)}, u32[]{:S(2)}) collective-permute-start(bf16[512,128]{1,0:T(8,128)(2,1)S(1)} %pad_maximum_fusion), channel_id=1, source_target_pairs={{32,0},{33,1},{34,2},{35,3},{36,4},{37,5},{38,6},{39,7},{40,8},{41... | collective-permute-start | bytes 393224 | tf_op jit(solution)/shard_map/ppermute | solution.py:31
  594.2 12.8 %collective-permute-start.4 = (f32[512,128]{1,0:T(8,128)S(1)}, f32[512,128]{1,0:T(8,128)S(1)}, u32[]{:S(2)}, u32[]{:S(2)}) collective-permute-start(f32[512,128]{1,0:T(8,128)S(1)} %get-tuple-element.732), channel_id=1, source_target_pairs={{0,32},{1,33},{2,34},{3,35},{4,36},{5,37},{6,38},{7,39},{8,40},{9,... | collective-permute-start | bytes 786440 | tf_op jit(solution)/shard_map/ppermute | solution.py:31
  595.5 11.4 %collective-permute-start.3 = (f32[512]{0:T(512)S(1)}, f32[512]{0:T(512)S(1)}, u32[]{:S(2)}, u32[]{:S(2)}) collective-permute-start(f32[512]{0:T(512)S(1)} %get-tuple-element.731), channel_id=1, source_target_pairs={{0,32},{1,33},{2,34},{3,35},{4,36},{5,37},{6,38},{7,39},{8,40},{9,... | collective-permute-start | bytes 6152 | tf_op jit(solution)/shard_map/ppermute | solution.py:31
  596.8 10.1 %collective-permute-start.5 = (f32[512]{0:T(512)S(1)}, f32[512]{0:T(512)S(1)}, u32[]{:S(2)}, u32[]{:S(2)}) collective-permute-start(f32[512]{0:T(512)S(1)} %get-tuple-element.734), channel_id=1, source_target_pairs={{0,32},{1,33},{2,34},{3,35},{4,36},{5,37},{6,38},{7,39},{8,40},{9,... | collective-permute-start | bytes 6152 | tf_op jit(solution)/shard_map/ppermute | solution.py:31
Sparse Core Ops, SparseCore 0:
  10.1 94.4 all-gather.9
  304.5 33.4 all-gather.7
  355.3 80.2 all-gather.5
where the time goes:
time: 621 us; the launch traced here: 615 us
  waiting for transfers between devices  246 us (40%)
  local copies, waits for them, and re-layouts  188 us (30%)
  matrix products  78.1 us (13%)
  other arithmetic  34.1 us (5%)
  starting transfers between devices  33.8 us (5%)
  between operations  13.5 us (2%)
  blocking collectives  12.5 us (2%)
  loops' own time  8.41 us (1%)
    all_gather x1, waiting for transfers between devices, turned_gather(): lax.all_gather(both, axis, axis=0, tiled=True)  91.2 us
    all_gather x1, waiting for transfers between devices, per_device(): arrived_rows = lax.all_gather(stacked, 'seq', axis=0, tiled=True)  70.4 us
    dynamic_slice x128, local copies, waits for them, and re-layouts, visit_one(): lax.dynamic_slice_in_dim(arrived_rows, block_index * sub_rows, sub_rows, 0)  61.2 us
    ppermute x11, waiting for transfers between devices, passed_along(): return lax.ppermute(block, axis, route)  51.2 us
    dot_general x6, matrix products, encoder_layer(): jnp.dot(hidden, w_out, preferred_element_type=jnp.float32)  45.1 us
    dynamic_slice x48, local copies, waits for them, and re-layouts, attend_block(): lax.dynamic_slice_in_dim(segment_ids, block_start, key_block.shape[0], 0)  36.7 us
    ppermute x11, starting transfers between devices, passed_along(): return lax.ppermute(block, axis, route)  33.6 us
    all_gather x1, waiting for transfers between devices, from_root(): lax.all_gather(x, axis)  33.4 us
  transfers between devices with their start and end apart: 14, of which 12 were waited for; matrix products, arithmetic and copies ran while one was open for 5% of the time, Pallas kernels for 0%

commit v1 on v0

--- a/solution.py
+++ b/solution.py
@@ -1,9 +1,241 @@
+import functools
 import math
 
 import jax
 import jax.numpy as jnp
 from jax import lax
+from jax.experimental import pallas as pl
+from jax.experimental.pallas import tpu as pltpu
 from jax.sharding import PartitionSpec as P
+
+NZ, NX, NC = 8, 4, 2
+
+
+def seq_id(z, x, c):
+    return lax.rem(z + NZ, NZ) * (NX * NC) + lax.rem(x + NX, NX) * NC + c
+
+
+class Ring:
+    def __init__(self, send_sem, recv_sem):
+        self.send_sem, self.recv_sem, self.used, self.live = send_sem, recv_sem, 0, []
+
+    def copy(self, sent, got, target):
+        n = self.used
+        self.used += 1
+        out = pltpu.make_async_remote_copy(
+            src_ref=sent, dst_ref=sent, send_sem=self.send_sem.at[n], recv_sem=self.recv_sem.at[n],
+            device_id={"seq": target}, device_id_type=pl.DeviceIdType.MESH)
+        into = pltpu.make_async_remote_copy(
+            src_ref=got, dst_ref=got, send_sem=self.send_sem.at[n], recv_sem=self.recv_sem.at[n],
+            device_id={"seq": target}, device_id_type=pl.DeviceIdType.MESH)
+        self.live.append(out)
+        return out, into
+
+    def finish(self):
+        for out in self.live:
+            out.wait_send()
+
+
+def greet(targets):
+    barrier = pltpu.get_barrier_semaphore()
+    for t in targets:
+        pl.semaphore_signal(barrier, inc=1, device_id={"seq": t}, device_id_type=pl.DeviceIdType.MESH)
+    pl.semaphore_wait(barrier, len(targets))
+
+
+def torus_gather(ring, me, a_one, a_many, b_one, b_many):
+    z, x, c = me
+    s = 1 - 2 * c
+    zm, zo = seq_id(z + s, x, c), seq_id(z - s, x, c)
+    xm, xo = seq_id(z, x + s, c), seq_id(z, x - s, c)
+    mate = seq_id(z, x, 1 - c)
+    zw = lambda k: lax.rem(z + k + 2 * NZ, NZ)
+    xw = lambda k: lax.rem(x + k + 2 * NX, NX)
+    ax_m = [ring.copy(a_one(z, xw(-k * s)), a_one(z, xw(-(k + 1) * s)), xm) for k in range(2)]
+    ax_o = ring.copy(a_one(z, x), a_one(z, xw(s)), xo)
+    bz_m = [ring.copy(b_one(zw(-k * s), x), b_one(zw(-(k + 1) * s), x), zm) for k in range(4)]
+    bz_o = [ring.copy(b_one(zw(k * s), x), b_one(zw((k + 1) * s), x), zo) for k in range(3)]
+    az_m = [ring.copy(a_many(zw(-k * s), c), a_many(zw(-(k + 1) * s), c), zm) for k in range(4)]
+    az_o = [ring.copy(a_many(zw(k * s), c), a_many(zw((k + 1) * s), c), zo) for k in range(3)]
+    bx_m = [ring.copy(b_many(xw(-k * s), c), b_many(xw(-(k + 1) * s), c), xm) for k in range(2)]
+    bx_o = ring.copy(b_many(x, c), b_many(xw(s), c), xo)
+    mates = []
+
+    def to_mate(sent, got):
+        pair = ring.copy(sent, got, mate)
+        pair[0].start()
+        mates.append(pair)
+
+    a_mate = lambda k: to_mate(a_many(zw(k * s), c), a_many(zw(-k * s), 1 - c))
+    b_mate = lambda k: to_mate(b_many(xw(k * s), c), b_many(xw(-k * s), 1 - c))
+
+    ax_m[0][0].start()
+    ax_o[0].start()
+    bz_m[0][0].start()
+    bz_o[0][0].start()
+    ax_m[0][1].wait_recv()
+    ax_m[1][0].start()
+    for k in range(3):
+        bz_m[k][1].wait_recv()
+        bz_m[k + 1][0].start()
+        bz_o[k][1].wait_recv()
+        if k < 2:
+            bz_o[k + 1][0].start()
+        if k == 1:
+            ax_o[1].wait_recv()
+            ax_m[1][1].wait_recv()
+    az_m[0][0].start()
+    az_o[0][0].start()
+    a_mate(0)
+    bz_m[3][1].wait_recv()
+    bx_m[0][0].start()
+    bx_o[0].start()
+    b_mate(0)
+    az_m[0][1].wait_recv()
+    az_m[1][0].start()
+    a_mate(-1)
+    az_o[0][1].wait_recv()
+    az_o[1][0].start()
+    a_mate(1)
+    bx_m[0][1].wait_recv()
+    bx_m[1][0].start()
+    b_mate(-1)
+    az_m[1][1].wait_recv()
+    az_m[2][0].start()
+    a_mate(-2)
+    az_o[1][1].wait_recv()
+    az_o[2][0].start()
+    a_mate(2)
+    bx_o[1].wait_recv()
+    b_mate(1)
+    az_m[2][1].wait_recv()
+    az_m[3][0].start()
+    a_mate(-3)
+    az_o[2][1].wait_recv()
+    a_mate(3)
+    bx_m[1][1].wait_recv()
+    b_mate(-2)
+    az_m[3][1].wait_recv()
+    a_mate(-4)
+    for pair in mates:
+        pair[1].wait_recv()
+
+
+GATHER_COPIES = 3 + 7 + 7 + 3 + 8 + 4
+
+
+def kv_gather_kernel(kv_ref, a_ref, b_ref, send_sem, recv_sem, own_sem):
+    me_seq = lax.axis_index("seq")
+    z, x, c = me_seq // (NX * NC), lax.rem(me_seq // NC, NX), lax.rem(me_seq, NC)
+    half = kv_ref.shape[0] // 2
+    mine = [
+        pltpu.make_async_copy(kv_ref.at[pl.ds(0, half)], a_ref.at[z, x, c], own_sem.at[0]),
+        pltpu.make_async_copy(kv_ref.at[pl.ds(half, half)], b_ref.at[z, x, c], own_sem.at[1]),
+    ]
+    for copy in mine:
+        copy.start()
+    greet([seq_id(z + 1, x, c), seq_id(z - 1, x, c), seq_id(z, x + 1, c), seq_id(z, x - 1, c), seq_id(z, x, 1 - c)])
+    for copy in mine:
+        copy.wait()
+    ring = Ring(send_sem, recv_sem)
+    torus_gather(
+        ring, (z, x, c),
+        lambda zz, xx: a_ref.at[zz, xx, c], lambda zz, cc: a_ref.at[zz, :, cc],
+        lambda zz, xx: b_ref.at[zz, xx, c], lambda xx, cc: b_ref.at[:, xx, cc])
+    ring.finish()
+
+
+def kv_gather(kv):
+    half = kv.shape[0] // 2
+    shape = jax.ShapeDtypeStruct((NZ, NX, NC, half, kv.shape[1]), kv.dtype)
+    return pl.pallas_call(
+        kv_gather_kernel,
+        out_shape=(shape, shape),
+        in_specs=[pl.BlockSpec(memory_space=pltpu.VMEM)],
+        out_specs=(pl.BlockSpec(memory_space=pltpu.VMEM),) * 2,
+        scratch_shapes=[
+            pltpu.SemaphoreType.DMA((GATHER_COPIES,)),
+            pltpu.SemaphoreType.DMA((GATHER_COPIES,)),
+            pltpu.SemaphoreType.DMA((2,)),
+        ],
+        compiler_params=pltpu.CompilerParams(collective_id=1, has_side_effects=True, vmem_limit_bytes=40 << 20),
+        cost_estimate=pl.CostEstimate(flops=0, bytes_accessed=40_000_000, transcendentals=0),
+        name="kv_gather",
+    )(kv)
+
+
+def flash_kernel(info_ref, q_ref, a_ref, b_ref, qseg_ref, aseg_ref, bseg_ref, o_ref):
+    shard = info_ref[0]
+    own_z = shard // 8
+    rows, head = q_ref.shape
+    keys = a_ref.shape[1]
+    half = keys // 8
+    q = q_ref[...]
+    qseg = qseg_ref[...]
+    row = lax.rem(lax.broadcasted_iota(jnp.int32, (rows, 1), 0), 128)
+    qpos = row + lax.rem(shard, 8) * 128
+    col = lax.broadcasted_iota(jnp.int32, (1, keys), 1)
+    kpos = (col // half) * 128 + lax.rem(col, half)
+    scale = 1.0 / math.sqrt(head)
+
+    def visit(carried, kv, kseg, extra):
+        top, total, acc = carried
+        s = lax.dot_general(q, kv[:, :head], (((1,), (1,)), ((), ())), preferred_element_type=jnp.float32)
+        allowed = kseg == qseg
+        if extra is not None:
+            allowed = allowed & extra
+        s = jnp.where(allowed, s * scale, -1e30)
+        new_top = jnp.maximum(top, jnp.max(s, axis=1, keepdims=True))
+        w = jnp.exp(s - new_top)
+        if extra is not None:
+            w = jnp.where(allowed, w, 0.0)
+        keep = jnp.exp(top - new_top)
+        total = total * keep + jnp.sum(w, axis=1, keepdims=True)
+        acc = acc * keep + jnp.dot(w.astype(jnp.bfloat16), kv[:, head:], preferred_element_type=jnp.float32)
+        return new_top, total, acc
+
+    state = (
+        jnp.full((rows, 1), -1e30, jnp.float32),
+        jnp.zeros((rows, 1), jnp.float32),
+        jnp.zeros((rows, head), jnp.float32),
+    )
+    state = visit(state, a_ref[own_z], aseg_ref[own_z], kpos <= qpos)
+    state = visit(state, b_ref[own_z], bseg_ref[own_z], kpos + half <= qpos)
+
+    def body(i, carried):
+        z = own_z - 1 - i
+        carried = visit(carried, a_ref[z], aseg_ref[z], None)
+        return visit(carried, b_ref[z], bseg_ref[z], None)
+
+    first_seg = info_ref[1]
+    count = jnp.int32(0)
+    for z in range(8):
+        count = count + ((z < own_z) & (info_ref[2 + z] >= first_seg)).astype(jnp.int32)
+    top, total, acc = lax.fori_loop(0, count, body, state)
+    o_ref[...] = (acc / total).astype(o_ref.dtype)
+
+
+def flash(q, a, b, segment_ids, shard, rows):
+    a = a.reshape(8, -1, a.shape[-1])
+    b = b.reshape(8, -1, b.shape[-1])
+    halves = segment_ids.reshape(8, 8, 2, 64)
+    aseg = halves[:, :, 0].reshape(8, 1, 512)
+    bseg = halves[:, :, 1].reshape(8, 1, 512)
+    own = lax.dynamic_slice_in_dim(segment_ids, shard * rows, rows, 0)
+    qseg = jnp.tile(own, q.shape[0] // rows)[:, None]
+    last = segment_ids.reshape(8, 1024)[:, -1]
+    info = jnp.concatenate([shard[None].astype(jnp.int32), own[:1], last])
+    whole = pl.BlockSpec(memory_space=pltpu.VMEM)
+    return pl.pallas_call(
+        flash_kernel,
+        out_shape=jax.ShapeDtypeStruct(q.shape, jnp.bfloat16),
+        in_specs=[pl.BlockSpec(memory_space=pltpu.SMEM)] + [whole] * 6,
+        out_specs=whole,
+        compiler_params=pltpu.CompilerParams(vmem_limit_bytes=48 << 20),
+        cost_estimate=pl.CostEstimate(flops=2 * 10**9, bytes_accessed=5_000_000, transcendentals=4_000_000),
+        name="flash",
+    )(info, q, a, b, qseg, aseg, bseg)
+
 
 GRID = 27
 
@@ -89,29 +321,6 @@
     is_valid = (offsets >= 0) & (offsets < upper_limit)
     picked = jnp.take(source, jnp.clip(offsets, 0, source.shape[0] - 1), axis=0)
     return (jnp.where(is_valid[:, None], picked, jnp.zeros((), source.dtype)), is_valid)
-
-
-def attend_block(softmax_state, queries, query_pos, query_seg, key_block, block_start, segment_ids):
-    row_top, row_total, row_acc = softmax_state
-    head_dim = queries.shape[1]
-    key_part = key_block[:, :head_dim]
-    value_part = key_block[:, head_dim:]
-    scores = lax.dot_general(
-        queries, key_part, (((1,), (1,)), ((), ())), preferred_element_type=jnp.float32
-    )
-    scores = scores * (1.0 / math.sqrt(head_dim))
-    key_pos = block_start + jnp.arange(key_block.shape[0], dtype=jnp.int32)
-    key_seg = lax.dynamic_slice_in_dim(segment_ids, block_start, key_block.shape[0], 0)
-    allowed = (key_pos[None, :] <= query_pos[:, None]) & (key_seg[None, :] == query_seg[:, None])
-    masked = jnp.where(allowed, scores, mask_floor)
-    new_top = jnp.maximum(row_top, jnp.max(masked, axis=1))
-    weights = jnp.where(allowed, jnp.exp(masked - new_top[:, None]), 0.0)
-    keep_old = jnp.exp(row_top - new_top)
-    row_total = row_total * keep_old + jnp.sum(weights, axis=1)
-    row_acc = row_acc * keep_old[:, None] + jnp.dot(
-        weights.astype(jnp.bfloat16), value_part, preferred_element_type=jnp.float32
-    )
-    return (new_top, row_total, row_acc)
 
 
 def per_device(
@@ -207,7 +416,6 @@
     queries = rotate(queries.reshape(shard_rows, group_size, head_size), positions).astype(
         jnp.bfloat16
     )
-    queries = queries.reshape(shard_rows * group_size, head_size)
     key_heads = jnp.dot(normed, key_weight, preferred_element_type=jnp.float32)
     key_heads = rotate(key_heads.reshape(shard_rows, 1, head_size), positions).astype(jnp.bfloat16)
     key_heads = key_heads.reshape(shard_rows, head_size)
@@ -215,81 +423,11 @@
         jnp.dot(normed, value_weight, preferred_element_type=jnp.float32) + value_bias
     ).astype(jnp.bfloat16)
     stacked = jnp.concatenate([key_heads, values], axis=1)
-    query_pos = jnp.repeat(positions, group_size)
-    query_seg = jnp.repeat(
-        lax.dynamic_slice_in_dim(segment_ids, shard_id * shard_rows, shard_rows, 0), group_size
-    )
-    query_total = shard_rows * group_size
-    blank_state = (
-        jnp.full((query_total,), mask_floor, jnp.float32),
-        jnp.zeros((query_total,), jnp.float32),
-        jnp.zeros((query_total, head_size), jnp.float32),
-    )
-    half_count = shard_count // 2
-    is_lower = shard_id < half_count
-    quarter = shard_count // 4
-    partner_queries = passed_along(queries, "seq", -half_count)
-    partner_id = shard_id + half_count
-    partner_pos = jnp.repeat(partner_id * shard_rows + local_slots, group_size)
-    partner_seg = jnp.repeat(
-        lax.dynamic_slice_in_dim(
-            segment_ids, jnp.minimum(partner_id, shard_count - 1) * shard_rows, shard_rows, 0
-        ),
-        group_size,
-    )
-    own_low = jnp.where(is_lower, 0, quarter * shard_rows)
-    own_high = (shard_id + 1) * shard_rows
-    part_high = jnp.where(is_lower, quarter * shard_rows, 0)
-
-    def visit_pair(pair_state, key_block, block_start):
-        own_state, other_state = pair_state
-        own_state = lax.cond(
-            (block_start >= own_low) & (block_start < own_high),
-            lambda carried: attend_block(
-                carried, queries, query_pos, query_seg, key_block, block_start, segment_ids
-            ),
-            lambda carried: carried,
-            own_state,
-        )
-        other_state = lax.cond(
-            block_start < part_high,
-            lambda carried: attend_block(
-                carried,
-                partner_queries,
-                partner_pos,
-                partner_seg,
-                key_block,
-                block_start,
-                segment_ids,
-            ),
-            lambda carried: carried,
-            other_state,
-        )
-        return (own_state, other_state)
-
-    initial = (blank_state, blank_state)
-    arrived_rows = lax.all_gather(stacked, "seq", axis=0, tiled=True)
-    sub_rows = math.gcd(arrived_rows.shape[0], shard_rows)
-
-    def visit_one(block_index, inner_state):
-        key_block = lax.dynamic_slice_in_dim(arrived_rows, block_index * sub_rows, sub_rows, 0)
-        return visit_pair(inner_state, key_block, block_index * sub_rows)
-
-    folded = lax.fori_loop(0, arrived_rows.shape[0] // sub_rows, visit_one, initial)
-    own_state, other_state = folded
-    back_top, back_total, back_acc = passed_along(
-        (other_state[0], other_state[1], other_state[2]), "seq", half_count
-    )
-    back_top = jnp.where(is_lower, mask_floor, back_top)
-    back_total = jnp.where(is_lower, 0.0, back_total)
-    back_acc = jnp.where(is_lower, 0.0, back_acc)
-    own_top, own_total, own_acc = own_state
-    row_top = jnp.maximum(own_top, back_top)
-    keep_own = jnp.exp(own_top - row_top)
-    keep_back = jnp.exp(back_top - row_top)
-    row_total = own_total * keep_own + back_total * keep_back
-    row_acc = own_acc * keep_own[:, None] + back_acc * keep_back[:, None]
-    attended = (row_acc / row_total[:, None]).astype(jnp.bfloat16)
+    queries = queries.reshape(shard_rows, group_size, head_size).transpose(1, 0, 2)
+    queries = queries.reshape(shard_rows * group_size, head_size)
+    half_a, half_b = kv_gather(stacked)
+    attended = flash(queries, half_a, half_b, segment_ids, shard_id, shard_rows)
+    attended = attended.reshape(group_size, shard_rows, head_size).transpose(1, 0, 2)
     return attended.reshape(shard_rows, group_size * head_size)
 
 

time: 621 us -> 418 us (0.67)
  the two profiles are of different devices: /device:TPU:231 before, /device:TPU:232 now
where the time goes in v1:
time: 418 us; the launch traced here: 413 us
  waiting for transfers between devices  169 us (40%)
  local copies, waits for them, and re-layouts  76 us (18%)
  matrix products  49.7 us (12%)
  Pallas kernels  42.1 us (10%)
  other arithmetic  26.2 us (6%)
  starting transfers between devices  22.4 us (5%)
  blocking collectives  14.4 us (3%)
  between operations  13.7 us (3%)
    all_gather x1, waiting for transfers between devices, turned_gather(): lax.all_gather(both, axis, axis=0, tiled=True)  92.5 us
    ppermute x7, waiting for transfers between devices, passed_along(): return lax.ppermute(block, axis, route)  51.9 us
    dot_general x6, matrix products, encoder_layer(): jnp.dot(hidden, w_out, preferred_element_type=jnp.float32)  45.1 us
    pallas_call x1, Pallas kernels, kv_gather(): pl.pallas_call(kv_gather_kernel, out_shape=(shape, shape), in_specs=[pl.B...  32.6 us
    all_gather x1, waiting for transfers between devices, from_root(): lax.all_gather(x, axis)  24.1 us
    ppermute x7, starting transfers between devices, passed_along(): return lax.ppermute(block, axis, route)  22.3 us
    dynamic_update_slice x6, local copies, waits for them, and re-layouts, run_tick(): lax.dynamic_update_slice_in_dim(collected, jnp.where(is_ready, result, cu...  20.7 us
    unnamed x25, local copies, waits for them, and re-layouts  18.6 us
  transfers between devices with their start and end apart: 9, of which 9 were waited for; matrix products, arithmetic and copies ran while one was open for 7% of the time, Pallas kernels for 0%

profile of v1, /device:TPU:232, one launch (start us, length us, event | category | flops | bytes accessed | tf_op | source)
XLA Modules:
  0.0 413.3 jit_solution(7525931166202116256)
XLA Ops:
  6.5 0.9 constant_dynamic-slice_fusion
  7.4 1.7 maximum_bitcast_fusion
  9.5 1.4 fusion.59
  10.8 1.4 fusion.60
  12.2 1.3 compare_and_fusion
  13.6 92.5 %all-gather.7.cloned.1.call-done = bf16[64,18,5248]{2,1,0:T(8,128)(2,1)} async-done(((bf16[1,18,5248]{2,1,0:T(8,128)(2,1)}), bf16[64,18,5248]{2,1,0:T(8,128)(2,1)}) %all-gather.7.cloned.1.call-update) | async-done | bytes 12091408 | tf_op jit(solution)/shard_map/all_gather | solution.py:252
  106.0 17.0 %reshape.295 = bf16[1152,5248]{1,0:T(8,128)(2,1)} reshape(bf16[64,18,5248]{2,1,0:T(8,128)(2,1)} %all-gather.7.cloned.1.call-done) | data formatting | bytes 24182784
  123.1 8.4 %slice_bitcast_fusion = (bf16[2176,1152]{0,1:T(8,128)(2,1)}, bf16[1152,2176]{1,0:T(8,128)(2,1)}) fusion(bf16[1152,5248]{1,0:T(8,128)(2,1)} %reshape.295), kind=kLoop, calls=%fused_computation.33 | loop fusion | bytes 20054016 | tf_op jit(solution)/shard_map/squeeze | solution.py:359
  131.4 8.4 %copy.39 = bf16[2176,1152]{1,0:T(8,128)(2,1)} copy(bf16[2176,1152]{0,1:T(8,128)(2,1)} %get-tuple-element.433) | data formatting | bytes 10027008 | tf_op jit(solution)/shard_map/while | solution.py:391
  139.9 1.3 broadcast_in_dim.79
  141.3 145.1 %while.19 = (s32[]{:T(128)}, bf16[243,1152]{1,0:T(8,128)(2,1)S(1)}, bf16[729,1152]{1,0:T(8,128)(2,1)}, pred[]{:T(512)}, bf16[729,1152]{1,0:T(8,128)(2,1)}, /*ind...) while((s32[]{:T(128)}, bf16[243,1152]{1,0:T(8,128)(2,1)S(1)}, ...), condition=%wide.region_3.4_spmd, body=%wide.region_0.3_spmd.sunk | while | flops 2446610432 | bytes 18521884 | solution.py:391
  141.3 1.4 convert_reduce_fusion.2
  143.1 7.5 %dynamic-slice_select_fusion.4 = (bf16[243,1152]{1,0:T(8,128)(2,1)S(1)}, bf16[243,1152]{1,0:T(8,128)(2,1)S(1)}) fusion(bf16[729,1152]{1,0:T(8,128)(2,1)} %get-tuple-element.544, s32[]{:T(128)S(6)} %select_n.157, pred[]{:T(512)S(6)} %and.70, f32[1152]{0:T(1024)S(1)} %reduce.18, bf16[2176,1152]{1,0:T(8,128)(2,1)} %get-tuple-element.569, ...), kind=kOutput, calls=%fused_computation.22.clone.1 | convolution fusion | flops 2444650496 | bytes 12880133 | tf_op jit(solution)/shard_map/while/body/eval_jaxpr/dot_general | solution.py:284
  150.6 3.4 collective-permute-start
  154.0 3.5 dynamic_update_slice.14
  157.5 10.1 %collective-permute-done = bf16[243,1152]{1,0:T(8,128)(2,1)S(1)} collective-permute-done((bf16[243,1152]{1,0:T(8,128)(2,1)S(1)}, bf16[243,1152]{1,0:T(8,128)(2,1)S(1)}, u32[]{:S(2)}, u32[]{:S(2)}) %collective-permute-start) | collective-permute-done | bytes 559904 | tf_op jit(solution)/shard_map/while/body/eval_jaxpr/ppermute | solution.py:263
  167.6 1.4 convert_reduce_fusion.2
  169.4 7.5 %dynamic-slice_select_fusion.4 = (bf16[243,1152]{1,0:T(8,128)(2,1)S(1)}, bf16[243,1152]{1,0:T(8,128)(2,1)S(1)}) fusion(bf16[729,1152]{1,0:T(8,128)(2,1)} %get-tuple-element.544, s32[]{:T(128)S(6)} %select_n.157, pred[]{:T(512)S(6)} %and.70, f32[1152]{0:T(1024)S(1)} %reduce.18, bf16[2176,1152]{1,0:T(8,128)(2,1)} %get-tuple-element.569, ...), kind=kOutput, calls=%fused_computation.22.clone.1 | convolution fusion | flops 2444650496 | bytes 12880133 | tf_op jit(solution)/shard_map/while/body/eval_jaxpr/dot_general | solution.py:284
  176.9 3.4 collective-permute-start
  180.3 3.5 dynamic_update_slice.14
  183.8 9.3 %collective-permute-done = bf16[243,1152]{1,0:T(8,128)(2,1)S(1)} collective-permute-done((bf16[243,1152]{1,0:T(8,128)(2,1)S(1)}, bf16[243,1152]{1,0:T(8,128)(2,1)S(1)}, u32[]{:S(2)}, u32[]{:S(2)}) %collective-permute-start) | collective-permute-done | bytes 559904 | tf_op jit(solution)/shard_map/while/body/eval_jaxpr/ppermute | solution.py:263
  193.1 1.4 convert_reduce_fusion.2
  194.9 7.5 %dynamic-slice_select_fusion.4 = (bf16[243,1152]{1,0:T(8,128)(2,1)S(1)}, bf16[243,1152]{1,0:T(8,128)(2,1)S(1)}) fusion(bf16[729,1152]{1,0:T(8,128)(2,1)} %get-tuple-element.544, s32[]{:T(128)S(6)} %select_n.157, pred[]{:T(512)S(6)} %and.70, f32[1152]{0:T(1024)S(1)} %reduce.18, bf16[2176,1152]{1,0:T(8,128)(2,1)} %get-tuple-element.569, ...), kind=kOutput, calls=%fused_computation.22.clone.1 | convolution fusion | flops 2444650496 | bytes 12880133 | tf_op jit(solution)/shard_map/while/body/eval_jaxpr/dot_general | solution.py:284
  202.4 3.4 collective-permute-start
  205.8 3.5 dynamic_update_slice.14
  209.3 8.4 %collective-permute-done = bf16[243,1152]{1,0:T(8,128)(2,1)S(1)} collective-permute-done((bf16[243,1152]{1,0:T(8,128)(2,1)S(1)}, bf16[243,1152]{1,0:T(8,128)(2,1)S(1)}, u32[]{:S(2)}, u32[]{:S(2)}) %collective-permute-start) | collective-permute-done | bytes 559904 | tf_op jit(solution)/shard_map/while/body/eval_jaxpr/ppermute | solution.py:263
  217.7 1.4 convert_reduce_fusion.2
  219.5 7.5 %dynamic-slice_select_fusion.4 = (bf16[243,1152]{1,0:T(8,128)(2,1)S(1)}, bf16[243,1152]{1,0:T(8,128)(2,1)S(1)}) fusion(bf16[729,1152]{1,0:T(8,128)(2,1)} %get-tuple-element.544, s32[]{:T(128)S(6)} %select_n.157, pred[]{:T(512)S(6)} %and.70, f32[1152]{0:T(1024)S(1)} %reduce.18, bf16[2176,1152]{1,0:T(8,128)(2,1)} %get-tuple-element.569, ...), kind=kOutput, calls=%fused_computation.22.clone.1 | convolution fusion | flops 2444650496 | bytes 12880133 | tf_op jit(solution)/shard_map/while/body/eval_jaxpr/dot_general | solution.py:284
  227.0 3.4 collective-permute-start
  230.4 3.5 dynamic_update_slice.14
  233.9 7.6 %collective-permute-done = bf16[243,1152]{1,0:T(8,128)(2,1)S(1)} collective-permute-done((bf16[243,1152]{1,0:T(8,128)(2,1)S(1)}, bf16[243,1152]{1,0:T(8,128)(2,1)S(1)}, u32[]{:S(2)}, u32[]{:S(2)}) %collective-permute-start) | collective-permute-done | bytes 559904 | tf_op jit(solution)/shard_map/while/body/eval_jaxpr/ppermute | solution.py:263
  241.4 1.4 convert_reduce_fusion.2
  243.2 7.5 %dynamic-slice_select_fusion.4 = (bf16[243,1152]{1,0:T(8,128)(2,1)S(1)}, bf16[243,1152]{1,0:T(8,128)(2,1)S(1)}) fusion(bf16[729,1152]{1,0:T(8,128)(2,1)} %get-tuple-element.544, s32[]{:T(128)S(6)} %select_n.157, pred[]{:T(512)S(6)} %and.70, f32[1152]{0:T(1024)S(1)} %reduce.18, bf16[2176,1152]{1,0:T(8,128)(2,1)} %get-tuple-element.569, ...), kind=kOutput, calls=%fused_computation.22.clone.1 | convolution fusion | flops 2444650496 | bytes 12880133 | tf_op jit(solution)/shard_map/while/body/eval_jaxpr/dot_general | solution.py:284
  250.8 3.4 collective-permute-start
  254.1 3.5 dynamic_update_slice.14
  257.6 6.7 %collective-permute-done = bf16[243,1152]{1,0:T(8,128)(2,1)S(1)} collective-permute-done((bf16[243,1152]{1,0:T(8,128)(2,1)S(1)}, bf16[243,1152]{1,0:T(8,128)(2,1)S(1)}, u32[]{:S(2)}, u32[]{:S(2)}) %collective-permute-start) | collective-permute-done | bytes 559904 | tf_op jit(solution)/shard_map/while/body/eval_jaxpr/ppermute | solution.py:263
  264.3 1.4 convert_reduce_fusion.2
  266.1 7.5 %dynamic-slice_select_fusion.4 = (bf16[243,1152]{1,0:T(8,128)(2,1)S(1)}, bf16[243,1152]{1,0:T(8,128)(2,1)S(1)}) fusion(bf16[729,1152]{1,0:T(8,128)(2,1)} %get-tuple-element.544, s32[]{:T(128)S(6)} %select_n.157, pred[]{:T(512)S(6)} %and.70, f32[1152]{0:T(1024)S(1)} %reduce.18, bf16[2176,1152]{1,0:T(8,128)(2,1)} %get-tuple-element.569, ...), kind=kOutput, calls=%fused_computation.22.clone.1 | convolution fusion | flops 2444650496 | bytes 12880133 | tf_op jit(solution)/shard_map/while/body/eval_jaxpr/dot_general | solution.py:284
  273.7 3.3 collective-permute-start
  277.0 3.4 dynamic_update_slice.14
  280.4 5.9 %collective-permute-done = bf16[243,1152]{1,0:T(8,128)(2,1)S(1)} collective-permute-done((bf16[243,1152]{1,0:T(8,128)(2,1)S(1)}, bf16[243,1152]{1,0:T(8,128)(2,1)S(1)}, u32[]{:S(2)}, u32[]{:S(2)}) %collective-permute-start) | collective-permute-done | bytes 559904 | tf_op jit(solution)/shard_map/while/body/eval_jaxpr/ppermute | solution.py:263
  286.3 2.5 reshape.260
  288.9 2.4 pad_convert_fusion
  291.2 5.5 %reshape.272 = f32[14,2,14,2,1152]{4,3,2,1,0:T(2,128)} reshape(f32[28,28,1152]{2,1,0:T(8,128)} %pad_convert_fusion) | data formatting | bytes 7225344 | tf_op jit(solution)/shard_map/reshape | solution.py:297
  296.7 4.5 %reduce_sum.58 = f32[14,14,1152]{2,1,0:T(8,128)S(1)} reduce(f32[14,2,14,2,1152]{4,3,2,1,0:T(2,128)} %reshape.272, f32[]{:T(128)} %constant.235.clone.1), dimensions={1,3}, to_apply=%region_4.5 | reduce | flops 677376 | bytes 4515844 | tf_op jit(solution)/shard_map/reduce_sum | solution.py:297
  301.5 0.9 gather_fusion.1
  302.6 2.1 collective-permute-start.1
  304.7 0.6 compare_and_fusion.1
  305.3 2.6 and_or_fusion
  307.9 0.9 gather_fusion
  308.8 3.9 collective-permute-done.1
  312.7 0.9 fusion.40
  315.0 24.1 %all-gather.5.cloned.1.call-done = bf16[512,1152]{1,0:T(8,128)(2,1)} async-done(((bf16[128,1152]{1,0:T(8,128)(2,1)}), bf16[512,1152]{1,0:T(8,128)(2,1)}) %all-gather.5.cloned.1.call-update) | async-done | bytes 1179664 | tf_op jit(solution)/shard_map/all_gather | solution.py:267
  339.1 2.2 fusion.35
  341.3 14.4 %all_gather.15 = bf16[128,3584]{1,0:T(8,128)(2,1)S(1)} all-gather(bf16[128,896]{1,0:T(8,128)(2,1)S(1)} %fusion.35), channel_id=1, replica_groups=mesh['section'=4,'seq'=64] {'section'}, dimensions={1}, use_global_device_ids=true | all-gather | bytes 1146880 | tf_op jit(solution)/shard_map/all_gather | solution.py:408
  356.0 0.5 convolution_bitcast_fusion
  356.9 0.5 fusion.38
  357.5 32.6 %kv_gather.1 = (bf16[8,4,2,64,256]{4,3,2,1,0:T(8,128)(2,1)S(1)}, bf16[8,4,2,64,256]{4,3,2,1,0:T(8,128)(2,1)S(1)}) custom-call(bf16[128,256]{1,0:T(8,128)(2,1)S(1)} %pad_maximum_fusion.1.kv_ref), custom_call_target="tpu_custom_call" | custom-call | bytes 40000000 | tf_op jit(solution)/shard_map/kv_gather/pallas_call | solution.py:151
  390.1 1.3 copy-done.1
  391.4 1.4 convolution_add_fusion.2
  392.8 1.7 reshape.263
  394.6 1.4 fusion.58
  396.3 9.5 %flash.1 = bf16[512,128]{1,0:T(8,128)(2,1)S(1)} custom-call(s32[10]{0:T(128)S(1)} %pad_add_fusion.info_ref, bf16[512,128]{1,0:T(8,128)(2,1)S(1)} %bitcast.47, bf16[8,512,256]{2,1,0:T(8,128)(2,1)S(1)} %bitcast.49, bf16[8,512,256]{2,1,0:T(8,128)(2,1)S(1)} %bitcast.50, s32[512,1]{1,0:T(8,128)S(1)} %copy.44.qseg_ref, s32[8,1,512]{2,1,0:T(1,128)S(1)} %reshape_squeeze.6.aseg_ref, ...), custom_call_target="tpu_custom_call" | custom-call | flops 2000000000 | bytes 5000000 | tf_op jit(solution)/shard_map/flash/pallas_call | solution.py:229
  405.8 0.7 copy.56
  (94 shorter events, 5.6 us)
Async XLA Ops:
  6.5 349.5 %copy-start = (bf16[3584,128]{1,0:T(8,128)(2,1)S(1)}, bf16[3584,128]{1,0:T(8,128)(2,1)}, u32[]{:S(2)}) copy-start(bf16[3584,128]{1,0:T(8,128)(2,1)} %param.35) | copy-start | bytes 2752516
  6.5 99.5 %all-gather.7.cloned.1.call-start = ((), (), s32[]{:S(2)}) async-start(), calls=%async_computation.1 | async-start | bytes 16373760 | tf_op jit(solution)/shard_map/all_gather | solution.py:252
  9.1 330.0 %all-gather.5.cloned.1.call-start = ((), (), s32[]{:S(2)}) async-start(), calls=%async_computation | async-start | bytes 1474560 | tf_op jit(solution)/shard_map/all_gather | solution.py:267
  139.9 1.4 copy-start.3
  139.9 1.4 copy-start.5
  139.9 1.4 copy-start.6
  150.6 17.0 %collective-permute-start = (bf16[243,1152]{1,0:T(8,128)(2,1)S(1)}, bf16[243,1152]{1,0:T(8,128)(2,1)S(1)}, u32[]{:S(2)}, u32[]{:S(2)}) collective-permute-start(bf16[243,1152]{1,0:T(8,128)(2,1)S(1)} %get-tuple-element.521), channel_id=1, source_target_pairs={{0,64},{64,128},{128,192},{1,65},{65,129},{129,193},{2,66},{66,130... | collective-permute-start | bytes 1679624 | tf_op jit(solution)/shard_map/while/body/eval_jaxpr/ppermute | solution.py:263
  176.9 16.1 %collective-permute-start = (bf16[243,1152]{1,0:T(8,128)(2,1)S(1)}, bf16[243,1152]{1,0:T(8,128)(2,1)S(1)}, u32[]{:S(2)}, u32[]{:S(2)}) collective-permute-start(bf16[243,1152]{1,0:T(8,128)(2,1)S(1)} %get-tuple-element.521), channel_id=1, source_target_pairs={{0,64},{64,128},{128,192},{1,65},{65,129},{129,193},{2,66},{66,130... | collective-permute-start | bytes 1679624 | tf_op jit(solution)/shard_map/while/body/eval_jaxpr/ppermute | solution.py:263
  202.4 15.3 %collective-permute-start = (bf16[243,1152]{1,0:T(8,128)(2,1)S(1)}, bf16[243,1152]{1,0:T(8,128)(2,1)S(1)}, u32[]{:S(2)}, u32[]{:S(2)}) collective-permute-start(bf16[243,1152]{1,0:T(8,128)(2,1)S(1)} %get-tuple-element.521), channel_id=1, source_target_pairs={{0,64},{64,128},{128,192},{1,65},{65,129},{129,193},{2,66},{66,130... | collective-permute-start | bytes 1679624 | tf_op jit(solution)/shard_map/while/body/eval_jaxpr/ppermute | solution.py:263
  227.0 14.4 %collective-permute-start = (bf16[243,1152]{1,0:T(8,128)(2,1)S(1)}, bf16[243,1152]{1,0:T(8,128)(2,1)S(1)}, u32[]{:S(2)}, u32[]{:S(2)}) collective-permute-start(bf16[243,1152]{1,0:T(8,128)(2,1)S(1)} %get-tuple-element.521), channel_id=1, source_target_pairs={{0,64},{64,128},{128,192},{1,65},{65,129},{129,193},{2,66},{66,130... | collective-permute-start | bytes 1679624 | tf_op jit(solution)/shard_map/while/body/eval_jaxpr/ppermute | solution.py:263
  250.8 13.5 %collective-permute-start = (bf16[243,1152]{1,0:T(8,128)(2,1)S(1)}, bf16[243,1152]{1,0:T(8,128)(2,1)S(1)}, u32[]{:S(2)}, u32[]{:S(2)}) collective-permute-start(bf16[243,1152]{1,0:T(8,128)(2,1)S(1)} %get-tuple-element.521), channel_id=1, source_target_pairs={{0,64},{64,128},{128,192},{1,65},{65,129},{129,193},{2,66},{66,130... | collective-permute-start | bytes 1679624 | tf_op jit(solution)/shard_map/while/body/eval_jaxpr/ppermute | solution.py:263
  273.7 12.7 %collective-permute-start = (bf16[243,1152]{1,0:T(8,128)(2,1)S(1)}, bf16[243,1152]{1,0:T(8,128)(2,1)S(1)}, u32[]{:S(2)}, u32[]{:S(2)}) collective-permute-start(bf16[243,1152]{1,0:T(8,128)(2,1)S(1)} %get-tuple-element.521), channel_id=1, source_target_pairs={{0,64},{64,128},{128,192},{1,65},{65,129},{129,193},{2,66},{66,130... | collective-permute-start | bytes 1679624 | tf_op jit(solution)/shard_map/while/body/eval_jaxpr/ppermute | solution.py:263
  302.5 11.1 %copy-start.4 = (s32[8192]{0:T(1024)S(1)}, s32[8192]{0:T(1024)}, u32[]{:S(2)}) copy-start(s32[8192]{0:T(1024)} %param.31) | copy-start | bytes 98308
  302.6 10.2 %collective-permute-start.1 = (bf16[128,1152]{1,0:T(8,128)(2,1)S(1)}, bf16[128,1152]{1,0:T(8,128)(2,1)S(1)}, u32[]{:S(2)}, u32[]{:S(2)}) collective-permute-start(bf16[128,1152]{1,0:T(8,128)(2,1)S(1)} %select_select_fusion), channel_id=1, source_target_pairs={{0,1},{1,2},{2,3},{3,4},{4,5},{5,6},{6,7},{7,8},{8,9},{9,10},{10,1... | collective-permute-start | bytes 884744 | tf_op jit(solution)/shard_map/ppermute | solution.py:263
  339.1 16.9 %copy-start.9 = (f32[3584]{0:T(1024)S(1)}, f32[3584]{0:T(1024)}, u32[]{:S(2)}) copy-start(f32[3584]{0:T(1024)} %param.32) | copy-start | bytes 43012
  355.7 1.2 copy-start.8
  355.7 1.2 copy-start.11
  356.0 35.4 %copy-start.7 = (bf16[3584,512]{1,0:T(8,128)(2,1)S(1)}, bf16[3584,512]{1,0:T(8,128)(2,1)}, u32[]{:S(2)}) copy-start(bf16[3584,512]{1,0:T(8,128)(2,1)} %param.33) | copy-start | bytes 11010052
  356.5 34.9 %copy-start.10 = (f32[512]{0:T(512)S(1)}, f32[512]{0:T(512)}, u32[]{:S(2)}) copy-start(f32[512]{0:T(512)} %param.34) | copy-start | bytes 6148
  390.1 1.3 copy-start.1
  394.6 1.7 copy-start.2
Sparse Core Ops, SparseCore 0:
  10.1 95.8 all-gather.6
  313.7 25.3 all-gather.4

commit v2 on v1

--- a/solution.py
+++ b/solution.py
@@ -19,15 +19,15 @@
     def __init__(self, send_sem, recv_sem):
         self.send_sem, self.recv_sem, self.used, self.live = send_sem, recv_sem, 0, []
 
-    def copy(self, sent, got, target):
+    def copy(self, sent, got, target, into=None):
         n = self.used
         self.used += 1
-        out = pltpu.make_async_remote_copy(
-            src_ref=sent, dst_ref=sent, send_sem=self.send_sem.at[n], recv_sem=self.recv_sem.at[n],
-            device_id={"seq": target}, device_id_type=pl.DeviceIdType.MESH)
-        into = pltpu.make_async_remote_copy(
-            src_ref=got, dst_ref=got, send_sem=self.send_sem.at[n], recv_sem=self.recv_sem.at[n],
-            device_id={"seq": target}, device_id_type=pl.DeviceIdType.MESH)
+        to = {"seq": target} if not isinstance(target, dict) else target
+        sems = dict(send_sem=self.send_sem.at[n], recv_sem=self.recv_sem.at[n])
+        make = functools.partial(
+            pltpu.make_async_remote_copy, device_id=to, device_id_type=pl.DeviceIdType.MESH, **sems)
+        out = make(src_ref=sent, dst_ref=sent if into is None else into)
+        into = make(src_ref=got, dst_ref=got)
         self.live.append(out)
         return out, into
 
@@ -39,7 +39,8 @@
 def greet(targets):
     barrier = pltpu.get_barrier_semaphore()
     for t in targets:
-        pl.semaphore_signal(barrier, inc=1, device_id={"seq": t}, device_id_type=pl.DeviceIdType.MESH)
+        t = {"seq": t} if not isinstance(t, dict) else t
+        pl.semaphore_signal(barrier, inc=1, device_id=t, device_id_type=pl.DeviceIdType.MESH)
     pl.semaphore_wait(barrier, len(targets))
 
 
@@ -59,66 +60,27 @@
     az_o = [ring.copy(a_many(zw(k * s), c), a_many(zw((k + 1) * s), c), zo) for k in range(3)]
     bx_m = [ring.copy(b_many(xw(-k * s), c), b_many(xw(-(k + 1) * s), c), xm) for k in range(2)]
     bx_o = ring.copy(b_many(x, c), b_many(xw(s), c), xo)
-    mates = []
-
-    def to_mate(sent, got):
-        pair = ring.copy(sent, got, mate)
-        pair[0].start()
-        mates.append(pair)
-
-    a_mate = lambda k: to_mate(a_many(zw(k * s), c), a_many(zw(-k * s), 1 - c))
-    b_mate = lambda k: to_mate(b_many(xw(k * s), c), b_many(xw(-k * s), 1 - c))
-
-    ax_m[0][0].start()
-    ax_o[0].start()
-    bz_m[0][0].start()
-    bz_o[0][0].start()
-    ax_m[0][1].wait_recv()
-    ax_m[1][0].start()
-    for k in range(3):
-        bz_m[k][1].wait_recv()
-        bz_m[k + 1][0].start()
-        bz_o[k][1].wait_recv()
-        if k < 2:
-            bz_o[k + 1][0].start()
-        if k == 1:
-            ax_o[1].wait_recv()
-            ax_m[1][1].wait_recv()
-    az_m[0][0].start()
-    az_o[0][0].start()
-    a_mate(0)
-    bz_m[3][1].wait_recv()
-    bx_m[0][0].start()
-    bx_o[0].start()
-    b_mate(0)
-    az_m[0][1].wait_recv()
-    az_m[1][0].start()
-    a_mate(-1)
-    az_o[0][1].wait_recv()
-    az_o[1][0].start()
-    a_mate(1)
-    bx_m[0][1].wait_recv()
-    bx_m[1][0].start()
-    b_mate(-1)
-    az_m[1][1].wait_recv()
-    az_m[2][0].start()
-    a_mate(-2)
-    az_o[1][1].wait_recv()
-    az_o[2][0].start()
-    a_mate(2)
-    bx_o[1].wait_recv()
-    b_mate(1)
-    az_m[2][1].wait_recv()
-    az_m[3][0].start()
-    a_mate(-3)
-    az_o[2][1].wait_recv()
-    a_mate(3)
-    bx_m[1][1].wait_recv()
-    b_mate(-2)
-    az_m[3][1].wait_recv()
-    a_mate(-4)
-    for pair in mates:
-        pair[1].wait_recv()
+    am = {k: ring.copy(a_many(zw(k * s), c), a_many(zw(-k * s), 1 - c), mate) for k in range(-4, 4)}
+    bm = {k: ring.copy(b_many(xw(k * s), c), b_many(xw(-k * s), 1 - c), mate) for k in range(-2, 2)}
+    go = lambda *pairs: [pair[0].start for pair in pairs]
+    on = lambda *pairs: [pair[1].wait_recv for pair in pairs]
+    return [
+        go(ax_m[0], ax_o, bz_m[0], bz_o[0]),
+        on(ax_m[0]) + go(ax_m[1]) + on(bz_m[0]) + go(bz_m[1]) + on(bz_o[0]) + go(bz_o[1]),
+        on(bz_m[1]) + go(bz_m[2]) + on(bz_o[1]) + go(bz_o[2]) + on(ax_o, ax_m[1]),
+        on(bz_m[2]) + go(bz_m[3]) + on(bz_o[2]) + go(az_m[0], az_o[0], am[0]),
+        on(bz_m[3]) + go(bx_m[0], bx_o, bm[0]),
+        on(az_m[0]) + go(az_m[1], am[-1]) + on(az_o[0]) + go(az_o[1], am[1]),
+        on(bx_m[0]) + go(bx_m[1], bm[-1]) + on(az_m[1]) + go(az_m[2], am[-2]) + on(az_o[1]) + go(az_o[2], am[2]),
+        on(bx_o) + go(bm[1]) + on(az_m[2]) + go(az_m[3], am[-3]) + on(az_o[2]) + go(am[3]),
+        on(bx_m[1]) + go(bm[-2]) + on(az_m[3]) + go(am[-4]),
+        on(*am.values(), *bm.values()),
+    ]
+
+
+def run(stage):
+    for step in stage:
+        step()
 
 
 GATHER_COPIES = 3 + 7 + 7 + 3 + 8 + 4
@@ -138,10 +100,11 @@
     for copy in mine:
         copy.wait()
     ring = Ring(send_sem, recv_sem)
-    torus_gather(
+    for stage in torus_gather(
         ring, (z, x, c),
         lambda zz, xx: a_ref.at[zz, xx, c], lambda zz, cc: a_ref.at[zz, :, cc],
-        lambda zz, xx: b_ref.at[zz, xx, c], lambda xx, cc: b_ref.at[:, xx, cc])
+        lambda zz, xx: b_ref.at[zz, xx, c], lambda xx, cc: b_ref.at[:, xx, cc]):
+        run(stage)
     ring.finish()
 
 
@@ -237,67 +200,237 @@
     )(info, q, a, b, qseg, aseg, bseg)
 
 
-GRID = 27
-
-
+CHUNKS, CHUNK = 8, 96
+ENC_COPIES = 7 + 7 + 2 * GATHER_COPIES + 8 + 1 + 6
 layer_eps = 1e-06
 rms_eps = 1e-06
 rope_base = 1000000.0
-mask_floor = -1e30
-
-
-def turned_gather(arrays, axis, dims):
-    turned = [jnp.moveaxis(a, dim, 0) for a, dim in zip(arrays, dims)]
-    both = jnp.concatenate([t.reshape(len(t), -1) for t in turned], axis=1)
-    filled, at, finished = (lax.all_gather(both, axis, axis=0, tiled=True), 0, [])
-    for t, dim in zip(turned, dims):
-        section = filled[:, at : at + t[0].size].reshape(-1, *t.shape[1:])
-        finished.append(jnp.moveaxis(section, 0, dim))
-        at += t[0].size
-    return tuple(finished)
-
-
-def passed_along(block, axis, distance):
-    devices = range(lax.axis_size(axis))
-    route = [(i - distance, i) for i in devices if i - distance in devices]
-    return lax.ppermute(block, axis, route)
-
-
-def from_root(x, axis, root):
-    return lax.dynamic_index_in_dim(lax.all_gather(x, axis), root, 0, keepdims=False)
-
-
-def layer_norm(values, scales):
-    widened = values.astype(jnp.float32)
-    center = widened - jnp.mean(widened, axis=-1, keepdims=True)
-    spread = jnp.mean(center * center, axis=-1, keepdims=True)
-    return center * lax.rsqrt(spread + layer_eps) * scales
-
-
-def encoder_layer(values, scales, w_in, b_in, w_out, b_out):
-    normed = layer_norm(values, scales).astype(jnp.bfloat16)
-    hidden = jax.nn.gelu(
-        jnp.dot(normed, w_in, preferred_element_type=jnp.float32) + b_in, approximate=True
-    ).astype(jnp.bfloat16)
-    summed = (
-        values.astype(jnp.float32)
-        + jnp.dot(hidden, w_out, preferred_element_type=jnp.float32)
-        + b_out
+
+
+def encoder_kernel(
+    w_ref, p_ref, pick_ref, patches_ref, gain_ref, bin_ref, bout_ref, select_ref, text_ref, valid_ref,
+    mixed_ref,
+    rec_w, rec_p, win, wout, extra, pa, pb, inflow, outflow, passed, vision, acc,
+    send_sem, recv_sem, chunk_send, chunk_recv, local_sem,
+):
+    me_seq, section = lax.axis_index("seq"), lax.axis_index("section")
+    z, x, c = me_seq // (NX * NC), lax.rem(me_seq // NC, NX), lax.rem(me_seq, NC)
+    j = lax.rem(me_seq, NX * NC)
+    last = section == 3
+    up, down = lax.rem(section + 1, 4), lax.rem(section + 3, 4)
+    shards = NZ * NX * NC
+    ahead, behind = lax.rem(me_seq + 1, shards), lax.rem(me_seq + shards - 1, shards)
+    others = [lax.rem(j + k, 8) for k in range(8)]
+    sources = [lax.rem(j + 8 - k, 8) for k in range(8)]
+    member = lambda k: z * (NX * NC) + k
+
+    own = [
+        pltpu.make_async_copy(w_ref.at[j], rec_w.at[j], local_sem.at[0]),
+        pltpu.make_async_copy(p_ref.at[j], rec_p.at[j], local_sem.at[1]),
+    ]
+    frame = pltpu.make_async_copy(patches_ref, inflow, local_sem.at[2])
+    for copy in own:
+        copy.start()
+
+    @pl.when(section == 0)
+    def _():
+        frame.start()
+
+    greet(
+        [member(k) for k in others[1:]]
+        + [seq_id(z + 1, x, c), seq_id(z - 1, x, c), ahead, behind, {"section": up}, {"section": down}]
     )
-    return summed.astype(jnp.bfloat16)
-
-
-def pool_frame(encoded):
-    channel = encoded.shape[-1]
-    grid_side = GRID
-    pool_side = (GRID + 1) // 2
-    grid_cells = encoded.astype(jnp.float32).reshape(grid_side, grid_side, channel)
-    pad_cells = 2 * pool_side - grid_side
-    grid_cells = jnp.pad(grid_cells, [(0, pad_cells), (0, pad_cells), (0, 0)])
-    totals = grid_cells.reshape(pool_side, 2, pool_side, 2, channel).sum(axis=(1, 3))
-    counts = jnp.minimum(2, grid_side - 2 * jnp.arange(pool_side)).astype(jnp.float32)
-    cell_area = counts[:, None] * counts[None, :]
-    return (totals / cell_area[..., None]).reshape(pool_side * pool_side, channel)
+    ring = Ring(send_sem, recv_sem)
+    spread_w = [ring.copy(w_ref.at[others[k]], rec_w.at[sources[k]], member(others[k]), rec_w.at[j]) for k in range(1, 8)]
+    spread_p = [ring.copy(p_ref.at[others[k]], rec_p.at[sources[k]], member(others[k]), rec_p.at[j]) for k in range(1, 8)]
+    for out, _ in spread_w:
+        out.start()
+    for copy in own:
+        copy.wait()
+    for _, into in spread_w:
+        into.wait_recv()
+    rows = win.shape[3]
+    block = jnp.dot(pick_ref[...], rec_w[...].reshape(-1, rec_w.shape[2]), preferred_element_type=jnp.float32)
+    block = block.astype(jnp.bfloat16)
+    wout[x, c, z] = block[:, 256:512]
+    win[x, c, z] = block[:, :256]
+    extra[c, z] = block[:, 512:]
+
+    def views(a, b):
+        return (
+            lambda zz, xx: a.at[xx, c, zz], lambda zz, cc: a.at[:, cc, zz],
+            lambda zz, xx: b.at[xx, c, zz], lambda xx, cc: b.at[xx, cc])
+
+    stages = torus_gather(ring, (z, x, c), *views(win, wout))
+    s = 1 - 2 * c
+    zw = lambda k: lax.rem(z + k + 2 * NZ, NZ)
+    zm, zo = seq_id(z + s, x, c), seq_id(z - s, x, c)
+    ez_m = [ring.copy(extra.at[c, zw(-k * s)], extra.at[c, zw(-(k + 1) * s)], zm) for k in range(4)]
+    ez_o = [ring.copy(extra.at[c, zw(k * s)], extra.at[c, zw((k + 1) * s)], zo) for k in range(3)]
+    e_mate = ring.copy(extra.at[c], extra.at[1 - c], seq_id(z, x, 1 - c))
+    for n, stage in enumerate(stages):
+        if n == 9:
+            e_mate[0].start()
+        run(stage)
+        if n == 3:
+            ez_m[0][0].start()
+            ez_o[0][0].start()
+        if 5 <= n < 9:
+            ez_m[n - 5][1].wait_recv()
+            if n < 8:
+                ez_m[n - 4][0].start()
+                ez_o[n - 5][1].wait_recv()
+            if n < 7:
+                ez_o[n - 4][0].start()
+    e_mate[1].wait_recv()
+    for out, _ in spread_p:
+        out.start()
+
+    def lay_out_p():
+        for _, into in spread_p:
+            into.wait_recv()
+        block = jnp.dot(pick_ref[...], rec_p[...].reshape(-1, rec_p.shape[2]), preferred_element_type=jnp.float32)
+        block = block.astype(jnp.bfloat16)
+        pa[x, c, z] = block[:, :256]
+        pb[x, c, z] = block[:, 256:]
+
+    p_stages = [[lay_out_p]] + torus_gather(ring, (z, x, c), *views(pa, pb))
+
+    @pl.when(last)
+    def _():
+        for stage in p_stages:
+            run(stage)
+
+    @pl.when(section == 0)
+    def _():
+        frame.wait()
+
+    def chunk_copy(i):
+        return pltpu.make_async_remote_copy(
+            src_ref=outflow.at[i], dst_ref=inflow.at[i], send_sem=chunk_send.at[i], recv_sem=chunk_recv.at[i],
+            device_id={"section": up}, device_id_type=pl.DeviceIdType.MESH)
+
+    def one_chunk(i, nothing):
+        @pl.when(section > 0)
+        def _():
+            chunk_copy(i).wait_recv()
+
+        widened = inflow[i].astype(jnp.float32)
+        center = widened - jnp.mean(widened, axis=1, keepdims=True)
+        spread = jnp.mean(center * center, axis=1, keepdims=True)
+        normed = (center * lax.rsqrt(spread + layer_eps) * gain_ref[...]).astype(jnp.bfloat16)
+        acc[...] = widened + bout_ref[...]
+
+        def part(w_in, b_in, w_out):
+            v = jnp.dot(normed, w_in, preferred_element_type=jnp.float32) + b_in
+            hidden = jax.nn.gelu(v, approximate=True).astype(jnp.bfloat16)
+            return lax.dot_general(hidden, w_out, (((1,), (1,)), ((), ())), preferred_element_type=jnp.float32)
+
+        for k in range(8):
+            flat = lambda ref: ref[k // 2, k % 2].reshape(8 * rows, 256)
+            acc[...] += part(flat(win), bin_ref[:, 256 * k : 256 * k + 256], flat(wout))
+        acc[...] += part(extra[0].reshape(8 * rows, 128), bin_ref[:, 2048:], extra[1].reshape(8 * rows, 128))
+        outflow[i] = acc[...].astype(jnp.bfloat16)
+
+        @pl.when(jnp.logical_not(last))
+        def _():
+            chunk_copy(i).start()
+
+        for n, stage in enumerate(p_stages[:CHUNKS]):
+            @pl.when((i == n) & jnp.logical_not(last))
+            def _():
+                run(stage)
+
+        return nothing
+
+    lax.fori_loop(0, CHUNKS, one_chunk, 0)
+
+    @pl.when(jnp.logical_not(last))
+    def _():
+        for stage in p_stages[CHUNKS:]:
+            run(stage)
+        for i in range(CHUNKS):
+            chunk_copy(i).wait_send()
+
+    half = vision.shape[2]
+    over = pltpu.make_async_remote_copy(
+        src_ref=passed.at[0], dst_ref=passed.at[1], send_sem=local_sem.at[3], recv_sem=local_sem.at[4],
+        device_id={"seq": ahead}, device_id_type=pl.DeviceIdType.MESH)
+    cast = lambda h, n, to: pltpu.make_async_remote_copy(
+        src_ref=vision.at[h], dst_ref=vision.at[h], send_sem=local_sem.at[5 + n], recv_sem=local_sem.at[9 + h],
+        device_id={"section": to}, device_id_type=pl.DeviceIdType.MESH)
+
+    @pl.when(last)
+    def _():
+        encoded = outflow[...].reshape(CHUNKS * CHUNK, outflow.shape[2])
+        count = select_ref.shape[0] // 2
+        passed[0] = jnp.dot(select_ref[count:], encoded, preferred_element_type=jnp.float32).astype(jnp.bfloat16)
+        over.start()
+        mine = jnp.dot(select_ref[:count], encoded, preferred_element_type=jnp.float32)
+        over.wait()
+        mine = mine + jnp.where(me_seq > 0, passed[1].astype(jnp.float32), 0.0)
+        mine = mine.astype(jnp.bfloat16)
+        vision[0] = mine[:, :half]
+        vision[1] = mine[:, half:]
+        copies = [cast(0, 0, 0), cast(1, 1, 2), cast(1, 2, 0), cast(0, 3, 2)]
+        for copy in copies:
+            copy.start()
+        for copy in copies:
+            copy.wait_send()
+
+    for me, first in ((0, 0), (2, 1)):
+        @pl.when(section == me)
+        def _():
+            cast(first, 0, 1).wait_recv()
+            on = cast(first, 0, 1)
+            on.start()
+            cast(1 - first, 0, 1).wait_recv()
+            on.wait_send()
+
+    @pl.when(section == 1)
+    def _():
+        cast(0, 0, 1).wait_recv()
+        cast(1, 0, 1).wait_recv()
+
+    left, right = vision[0], vision[1]
+    valid = valid_ref[...] > 0
+    for k in range(7):
+        for n, ref in enumerate((pa, pb)):
+            w = ref[k // 2, k % 2].reshape(8 * rows, 256)
+            out = jnp.dot(left, w[:half], preferred_element_type=jnp.float32)
+            out = out + jnp.dot(right, w[half:], preferred_element_type=jnp.float32)
+            at = 512 * k + 256 * n
+            mixed_ref[:, at : at + 256] = jnp.where(
+                valid, out.astype(jnp.bfloat16), text_ref[:, at : at + 256])
+    ring.finish()
+
+
+def encode(w, p, patches, gain, b_in, b_out, select, text, valid):
+    rows, width = w.shape[1] and 144, patches.shape[2]
+    at = jnp.arange(rows)[:, None]
+    pick = (jnp.arange(256)[None, :] == 32 * (at // 18) + at % 18).astype(jnp.bfloat16)
+    whole = pl.BlockSpec(memory_space=pltpu.VMEM)
+    bf = jnp.bfloat16
+    big = pltpu.VMEM((NX, NC, NZ, rows, 256), bf)
+    return pl.pallas_call(
+        encoder_kernel,
+        out_shape=jax.ShapeDtypeStruct(text.shape, bf),
+        in_specs=[whole, whole, whole, pl.BlockSpec(memory_space=pl.ANY)] + [whole] * 6,
+        out_specs=whole,
+        scratch_shapes=[
+            pltpu.VMEM(w.shape, bf), pltpu.VMEM(p.shape, bf),
+            big, big, pltpu.VMEM((NC, NZ, rows, 128), bf), big, big,
+            pltpu.VMEM((CHUNKS, CHUNK, width), bf), pltpu.VMEM((CHUNKS, CHUNK, width), bf),
+            pltpu.VMEM((2, text.shape[0], width), bf), pltpu.VMEM((2, text.shape[0], width // 2), bf),
+            pltpu.VMEM((CHUNK, width), jnp.float32),
+            pltpu.SemaphoreType.DMA((ENC_COPIES,)), pltpu.SemaphoreType.DMA((ENC_COPIES,)),
+            pltpu.SemaphoreType.DMA((CHUNKS,)), pltpu.SemaphoreType.DMA((CHUNKS,)),
+            pltpu.SemaphoreType.DMA((12,)),
+        ],
+        compiler_params=pltpu.CompilerParams(collective_id=0, has_side_effects=True, vmem_limit_bytes=60 << 20),
+        cost_estimate=pl.CostEstimate(flops=10**10, bytes_accessed=40_000_000, transcendentals=2_000_000),
+        name="encode",
+    )(w, p, pick, patches, gain, b_in, b_out, select, text, valid)
 
 
 def rotate(values, positions):
@@ -317,10 +450,14 @@
     )
 
 
-def take_rows(source, offsets, upper_limit):
-    is_valid = (offsets >= 0) & (offsets < upper_limit)
-    picked = jnp.take(source, jnp.clip(offsets, 0, source.shape[0] - 1), axis=0)
-    return (jnp.where(is_valid[:, None], picked, jnp.zeros((), source.dtype)), is_valid)
+def pool_rows(offsets, count):
+    patch = jnp.arange(CHUNKS * CHUNK, dtype=jnp.int32)
+    down, across = patch // 27, patch % 27
+    cell = jnp.where(patch < 729, (down // 2) * 14 + across // 2, -1)
+    share = jnp.where(down == 26, 1.0, 0.5) * jnp.where(across == 26, 1.0, 0.5)
+    is_valid = (offsets >= 0) & (offsets < count)
+    hit = is_valid[:, None] & (offsets[:, None] == cell[None, :])
+    return jnp.where(hit, share[None, :], 0.0).astype(jnp.bfloat16), is_valid
 
 
 def per_device(
@@ -342,70 +479,34 @@
     value_weight,
     value_bias,
 ):
-    section_count = lax.axis_size("section")
-    section_id = lax.axis_index("section")
-    shard_count = lax.axis_size("seq")
     shard_id = lax.axis_index("seq")
     shard_rows = text_embed.shape[0]
-    model_width = text_embed.shape[1]
     head_size = key_weight.shape[1]
     group_size = query_weight.shape[1] // head_size
-    frame_patches = patches[0]
-    patch_rows, feature_width = frame_patches.shape
-    column_count = model_width // section_count
-    proj_block = lax.dynamic_slice_in_dim(proj_weight, section_id * column_count, column_count, 1)
-    w_in, w_out, proj_full = turned_gather((fc_in, fc_out, proj_block), "seq", (1, 2, 0))
-    w_in = w_in[0]
-    w_out = w_out[0]
-    layer_gain = fc_gain[0]
-    bias_in = fc_in_bias[0]
-    bias_out = fc_out_bias[0]
-    band_rows = 9
-    batch_rows = band_rows * GRID
-    batches = GRID // band_rows
-    tick_count = batches + section_count - 1
-    first_section = section_id == 0
-    last_section = section_id == section_count - 1
-
-    def run_tick(tick_index, loop_carry):
-        inflow, collected = loop_carry
-        feed_rows = lax.dynamic_slice_in_dim(
-            frame_patches, jnp.minimum(tick_index, batches - 1) * batch_rows, batch_rows, 0
-        )
-        result = encoder_layer(
-            jnp.where(first_section, feed_rows, inflow), layer_gain, w_in, bias_in, w_out, bias_out
-        )
-        slot_start = jnp.clip(tick_index - section_count + 1, 0, batches - 1) * batch_rows
-        current = lax.dynamic_slice_in_dim(collected, slot_start, batch_rows, 0)
-        is_ready = last_section & (tick_index >= section_count - 1)
-        collected = lax.dynamic_update_slice_in_dim(
-            collected, jnp.where(is_ready, result, current), slot_start, 0
-        )
-        inflow = passed_along(result, "section", 1)
-        return (inflow, collected)
-
-    start_state = (
-        jnp.zeros((batch_rows, feature_width), jnp.bfloat16),
-        jnp.zeros((patch_rows, feature_width), jnp.bfloat16),
-    )
-    inflow, collected = lax.fori_loop(0, tick_count, run_tick, start_state)
-    pooled = pool_frame(collected).astype(jnp.bfloat16)
+
+    def pieces(matrix, width):
+        matrix = jnp.pad(matrix, [(0, 32 - matrix.shape[0]), (0, 8 * width - matrix.shape[1])])
+        return matrix.reshape(32, 8, width).transpose(1, 0, 2)
+
+    w_in, w_out = fc_in[0], fc_out[0].T
+    tail = jnp.stack([w_in[:, 2048:], w_out[:, 2048:]])
+    tail = jnp.pad(jnp.tile(tail, (4, 1, 1)), [(0, 0), (0, 14), (0, 0)])
+    w = jnp.concatenate([pieces(w_in[:, :2048], 256), pieces(w_out[:, :2048], 256), tail], axis=2)
+    p = pieces(proj_weight, 512)
+    frame = jnp.pad(patches[0], [(0, CHUNKS * CHUNK - patches.shape[1]), (0, 0)])
+    frame = frame.reshape(CHUNKS, CHUNK, patches.shape[2])
+
     local_slots = jnp.arange(shard_rows, dtype=jnp.int32)
     positions = shard_id * shard_rows + local_slots
-    own_start = frame_start[shard_id]
-    own_count = frame_count[shard_id]
     previous = jnp.maximum(shard_id - 1, 0)
     prev_offsets = positions - frame_start[previous]
     prev_valid = (shard_id > 0) & (prev_offsets >= 0) & (prev_offsets < frame_count[previous])
-    own_rows, own_valid = take_rows(pooled, positions - own_start, own_count)
-    sent_rows, sent_valid = take_rows(pooled, positions + shard_rows - own_start, own_count)
-    arrived = passed_along(sent_rows, "seq", 1)
-    vision = jnp.where(own_valid[:, None], own_rows, arrived)
-    vision = from_root(vision, "section", section_count - 1)
-    block_cols = jnp.dot(vision, proj_full, preferred_element_type=jnp.float32).astype(jnp.bfloat16)
-    text_cols = lax.dynamic_slice_in_dim(text_embed, section_id * column_count, column_count, 1)
-    mixed_cols = jnp.where((own_valid | prev_valid)[:, None], block_cols, text_cols)
-    inputs = lax.all_gather(mixed_cols, "section", axis=1, tiled=True)
+    own_offsets = positions - frame_start[shard_id]
+    own_pool, own_valid = pool_rows(own_offsets, frame_count[shard_id])
+    next_pool, _ = pool_rows(own_offsets + shard_rows, frame_count[shard_id])
+    select = jnp.concatenate([own_pool, next_pool])
+    valid = (own_valid | prev_valid).astype(jnp.int32)[:, None]
+    inputs = encode(w, p, frame, fc_gain, fc_in_bias, fc_out_bias, select, text_embed, valid)
     widened = inputs.astype(jnp.float32)
     normed = (
         widened

time: 418 us -> 216 us (0.52)
  waiting for transfers between devices: 169 us -> 0 us
  Pallas kernels: 42.1 us -> 191 us
  local copies, waits for them, and re-layouts: 76 us -> 10.3 us
  matrix products: 49.7 us -> 2.99 us
  starting transfers between devices: 22.4 us -> 0 us
  other arithmetic: 26.2 us -> 10.3 us
  blocking collectives: 14.4 us -> 0 us
  between operations: 13.7 us -> 0.29 us
    pallas_call x0 -> x1, Pallas kernels: none -> 150 us  [encode(): pl.pallas_call(encoder_kernel, out_shape=jax.ShapeDtypeStruct(text.shape,...]
    all_gather x2 -> x0, waiting for transfers between devices: 117 us -> none  [the longest x1 92.5 us: turned_gather(): lax.all_gather(both, axis, axis=0, tiled=True)]
    ppermute x7 -> x0, waiting for transfers between devices: 51.9 us -> none  [passed_along(): return lax.ppermute(block, axis, route)]
    dot_general x7 -> x0, matrix products: 47.3 us -> none  [the longest x6 45.1 us: encoder_layer(): jnp.dot(hidden, w_out, preferred_element_type=jnp.float32)]
    ppermute x7 -> x0, starting transfers between devices: 22.3 us -> none  [passed_along(): return lax.ppermute(block, axis, route)]
    dynamic_update_slice x6 -> x0, local copies, waits for them, and re-layouts: 20.7 us -> none  [run_tick(): lax.dynamic_update_slice_in_dim(collected, jnp.where(is_ready, result, cu...]
    unnamed x25 -> x18, local copies, waits for them, and re-layouts: 18.6 us -> 0.04 us
    reduce_sum x13 -> x0, other arithmetic: 14.6 us -> none  [the longest x6 8.34 us: layer_norm(): center = widened - jnp.mean(widened, axis=-1, keepdims=True)]
  transfers between devices with their start and end apart: 9 -> 0, of which waited for: 9 -> 0; matrix products, arithmetic and copies ran while one was open for 7% -> 0% of each run, Pallas kernels for 0% -> 0%
where the time goes in v2:
time: 216 us; the launch traced here: 214 us
  Pallas kernels  191 us (88%)
  local copies, waits for them, and re-layouts  10.3 us (5%)
  other arithmetic  10.3 us (5%)
  matrix products  2.99 us (1%)
    pallas_call x1, Pallas kernels, encode(): pl.pallas_call(encoder_kernel, out_shape=jax.ShapeDtypeStruct(text.shape,...  150 us
    pallas_call x1, Pallas kernels, kv_gather(): pl.pallas_call(kv_gather_kernel, out_shape=(shape, shape), in_specs=[pl.B...  31.3 us
    pallas_call x1, Pallas kernels, flash(): pl.pallas_call(flash_kernel, out_shape=jax.ShapeDtypeStruct(q.shape, jnp....  9.49 us

profile of v2, /device:TPU:232, one launch (start us, length us, event | category | flops | bytes accessed | tf_op | source)
XLA Modules:
  0.0 214.4 jit_solution(9016679124839334222)
XLA Ops:
  0.0 0.0 copy-start
  0.0 0.0 copy-start.3
  0.0 0.8 dynamic_slice.16
  0.9 1.4 fusion.57
  2.3 1.3 compare_and_fusion.1
  3.6 0.6 compare_and_fusion
  4.3 0.7 slice_bitcast_fusion
  5.0 0.8 reshape.319
  5.8 0.2 slice_reduce_fusion.2
  6.0 0.1 pad_add_fusion.info_ref
  6.1 3.2 %fusion.24.valid_ref = s32[128,1]{1,0:T(8,128)} fusion(s32[]{:T(128)S(6)} %mul.143, s32[]{:T(128)} %bitcast.16, s32[]{:T(128)} %bitcast.15, s32[]{:T(128)} %bitcast.14, s32[]{:T(128)} %bitcast.13, pred[]{:T(512)S(6)} %gt.3), kind=kLoop, calls=%fused_computation.47 | loop fusion | flops 1536 | bytes 533 | tf_op jit(solution)/shard_map/convert_element_type | solution.py:508
  9.3 0.9 reshape.329
  10.2 0.2 slice_reduce_fusion
  10.3 0.1 reshape_squeeze.7.bseg_ref
  10.4 0.1 reshape_squeeze.6.aseg_ref
  10.5 0.7 fusion.6.pick_ref
  11.2 0.9 slice.49
  12.2 0.9 slice.50
  13.1 0.0 copy-start.1
  13.1 0.8 fusion.5.w_ref
  13.9 0.3 multiply_cosine_fusion.1
  14.2 0.1 copy.49.qseg_ref
  14.3 0.0 copy-done.3
  14.4 0.7 copy.70
  15.1 0.2 select_convert_fusion.1
  15.3 0.8 pad_maximum_fusion.select_ref
  16.1 0.0 copy-done.1
  16.1 1.4 pad.23
  17.5 0.0 copy-start.6
  17.5 0.0 copy-start.8
  17.5 149.9 %encode.1 = bf16[128,3584]{1,0:T(8,128)(2,1)} custom-call(bf16[8,32,640]{2,1,0:T(8,128)(2,1)} %fusion.5.w_ref, bf16[8,32,512]{2,1,0:T(8,128)(2,1)} %bitcast.65, bf16[144,256]{1,0:T(8,128)(2,1)} %fusion.6.pick_ref, bf16[8,96,1152]{2,1,0:T(8,128)(2,1)} %bitcast.60, f32[1,1152]{1,0:T(1,128)} %gain_ref.1, f32[1,2176]{1,0:T(1,128)} %bin_ref.1, ...), custom_call_target="tpu_custom_call" | custom-call | flops 10000000000 | bytes 40000000 | tf_op jit(solution)/shard_map/encode/pallas_call | solution.py:415
  167.4 0.0 copy-start.2
  167.4 0.0 copy-start.5
  167.4 1.6 fusion
  169.0 0.0 copy-done
  169.0 0.0 copy-done.6
  169.0 0.0 copy-done.8
  169.0 0.0 copy-start.4
  169.0 0.0 copy-start.7
  169.0 1.8 fusion.3
  170.8 0.0 copy-done.2
  170.8 0.0 copy-done.5
  170.9 0.5 convolution_bitcast_fusion
  171.3 0.0 copy-done.4
  171.4 0.0 copy-done.7
  171.4 0.7 convolution_add_fusion
  172.1 0.3 fusion.27
  172.4 0.1 pad_maximum_fusion.2.kv_ref
  172.5 0.1 reshape.324
  172.6 0.2 fusion.56
  172.8 0.1 subtract_convert_fusion
  172.9 0.1 pad_maximum_fusion.1
  173.0 31.3 %kv_gather.1 = (bf16[8,4,2,64,256]{4,3,2,1,0:T(8,128)(2,1)S(1)}, bf16[8,4,2,64,256]{4,3,2,1,0:T(8,128)(2,1)S(1)}) custom-call(bf16[128,256]{1,0:T(8,128)(2,1)S(1)} %pad_maximum_fusion.2.kv_ref), custom_call_target="tpu_custom_call" | custom-call | bytes 40000000 | tf_op jit(solution)/shard_map/kv_gather/pallas_call | solution.py:114
  204.3 9.5 %flash.1 = bf16[512,128]{1,0:T(8,128)(2,1)S(1)} custom-call(s32[10]{0:T(128)S(1)} %pad_add_fusion.info_ref, bf16[512,128]{1,0:T(8,128)(2,1)S(1)} %bitcast.56, bf16[8,512,256]{2,1,0:T(8,128)(2,1)S(1)} %bitcast.58, bf16[8,512,256]{2,1,0:T(8,128)(2,1)S(1)} %bitcast.59, s32[512,1]{1,0:T(8,128)S(1)} %copy.49.qseg_ref, s32[8,1,512]{2,1,0:T(1,128)S(1)} %reshape_squeeze.6.aseg_ref, ...), custom_call_target="tpu_custom_call" | custom-call | flops 2000000000 | bytes 5000000 | tf_op jit(solution)/shard_map/flash/pallas_call | solution.py:192
  213.8 0.7 copy.71
  (14 shorter events, 0.2 us)
Async XLA Ops:
  0.0 169.0 %copy-start = (bf16[3584,128]{1,0:T(8,128)(2,1)S(1)}, bf16[3584,128]{1,0:T(8,128)(2,1)}, u32[]{:S(2)}) copy-start(bf16[3584,128]{1,0:T(8,128)(2,1)} %param.32) | copy-start | bytes 2752516
  0.0 14.3 %copy-start.3 = (bf16[18,3584]{1,0:T(8,128)(2,1)S(1)}, bf16[18,3584]{1,0:T(8,128)(2,1)}, u32[]{:S(2)}) copy-start(bf16[18,3584]{1,0:T(8,128)(2,1)} %param.23) | copy-start | bytes 387076
  13.1 3.0 %copy-start.1 = (bf16[1,729,1152]{2,1,0:T(8,128)(2,1)S(1)}, bf16[1,729,1152]{2,1,0:T(8,128)(2,1)}, u32[]{:S(2)}) copy-start(bf16[1,729,1152]{2,1,0:T(8,128)(2,1)} %param.17) | copy-start | bytes 5038852
  17.5 151.5 %copy-start.6 = (f32[3584]{0:T(1024)S(1)}, f32[3584]{0:T(1024)}, u32[]{:S(2)}) copy-start(f32[3584]{0:T(1024)} %param.28) | copy-start | bytes 43012
  17.5 151.5 %copy-start.8 = (f32[128]{0:T(128)S(1)}, f32[128]{0:T(128)}, u32[]{:S(2)}) copy-start(f32[128]{0:T(128)} %param.33) | copy-start | bytes 1540
  167.4 3.5 %copy-start.2 = (bf16[128,3584]{1,0:T(8,128)(2,1)S(1)}, bf16[128,3584]{1,0:T(8,128)(2,1)}, u32[]{:S(2)}) copy-start(bf16[128,3584]{1,0:T(8,128)(2,1)} %encode.1) | copy-start | bytes 2752516
  167.4 3.5 %copy-start.5 = (bf16[3584,128]{1,0:T(8,128)(2,1)S(1)}, bf16[3584,128]{1,0:T(8,128)(2,1)}, u32[]{:S(2)}) copy-start(bf16[3584,128]{1,0:T(8,128)(2,1)} %param.31) | copy-start | bytes 2752516
  169.0 2.3 %copy-start.4 = (bf16[3584,512]{1,0:T(8,128)(2,1)S(1)}, bf16[3584,512]{1,0:T(8,128)(2,1)}, u32[]{:S(2)}) copy-start(bf16[3584,512]{1,0:T(8,128)(2,1)} %param.29) | copy-start | bytes 11010052
  169.0 2.3 %copy-start.7 = (f32[512]{0:T(512)S(1)}, f32[512]{0:T(512)}, u32[]{:S(2)}) copy-start(f32[512]{0:T(512)} %param.30) | copy-start | bytes 6148

commit v3 on v2

v3 whole, which is shorter than its diff:
```python
import functools
import math

import jax
import jax.numpy as jnp
from jax import lax
from jax.experimental import pallas as pl
from jax.experimental.pallas import tpu as pltpu
from jax.sharding import PartitionSpec as P

NZ, NX, NC = 8, 4, 2


def seq_id(z, x, c):
    return lax.rem(z + NZ, NZ) * (NX * NC) + lax.rem(x + NX, NX) * NC + c


class Ring:
    def __init__(self, send_sem, recv_sem):
        self.send_sem, self.recv_sem, self.used, self.live = send_sem, recv_sem, 0, []

    def copy(self, sent, got, target, into=None):
        n = self.used
        self.used += 1
        to = {"seq": target} if not isinstance(target, dict) else target
        sems = dict(send_sem=self.send_sem.at[n], recv_sem=self.recv_sem.at[n])
        make = functools.partial(
            pltpu.make_async_remote_copy, device_id=to, device_id_type=pl.DeviceIdType.MESH, **sems)
        out = make(src_ref=sent, dst_ref=sent if into is None else into)
        into = make(src_ref=got, dst_ref=got)
        self.live.append(out)
        return out, into

    def finish(self):
        for out in self.live:
            out.wait_send()


def greet(targets):
    barrier = pltpu.get_barrier_semaphore()
    for t in targets:
        t = {"seq": t} if not isinstance(t, dict) else t
        pl.semaphore_signal(barrier, inc=1, device_id=t, device_id_type=pl.DeviceIdType.MESH)
    pl.semaphore_wait(barrier, len(targets))


def torus_gather(ring, me, a_one, a_many, b_one, b_many, b_like_a=False):
    z, x, c = me
    s = 1 - 2 * c
    zm, zo = seq_id(z + s, x, c), seq_id(z - s, x, c)
    xm, xo = seq_id(z, x + s, c), seq_id(z, x - s, c)
    mate = seq_id(z, x, 1 - c)
    zw = lambda k: lax.rem(z - k * s + 2 * NZ, NZ)
    xw = lambda k: lax.rem(x - k * s + 2 * NX, NX)
    one = {"a": lambda dx, dz: a_one(zw(dz), xw(dx)), "b": lambda dx, dz: b_one(zw(dz), xw(dx))}
    dxs, dzs = (0, 1, -1, 2), (0, 1, -1, 2, -2, 3, -3, 4)
    keys = sorted(
        ((kind, dx, dz) for kind in "ab" for dx in dxs for dz in dzs),
        key=lambda k: (abs(k[1]) + abs(k[2]), k[2 if k[0] == "a" else 1] != 0))
    toward = lambda d: d - 1 if d > 0 else d + 1
    copies, after = {}, {key: [] for key in keys}
    for key in keys:
        kind, dx, dz = key
        along_z = dz != 0 and (kind == "a" or dx == 0)
        if dx == dz == 0:
            continue
        source = (dx, toward(dz)) if along_z else (toward(dx), dz)
        target = (zm if dz > 0 else zo) if along_z else (xm if dx > 0 else xo)
        copies[key] = ring.copy(one[kind](*source), one[kind](dx, dz), target)
        after[(kind, *source)].append(copies[key])
    am = {d: ring.copy(a_many(zw(d), c), a_many(zw(-d), 1 - c), mate) for d in dzs}
    bw, bds, late = (zw, dzs, 2) if b_like_a else (xw, dxs, 4)
    bm = {d: ring.copy(b_many(bw(d), c), b_many(bw(-d), 1 - c), mate) for d in bds}
    stages = []
    for t in range(7):
        stage = []
        for key in keys:
            if abs(key[1]) + abs(key[2]) == t:
                if t:
                    stage.append(copies[key][1].wait_recv)
                stage += [out.start for out, _ in after[key]]
        stage += [am[d][0].start for d in dzs if abs(d) + 2 == t]
        stage += [bm[d][0].start for d in bds if abs(d) + late == t]
        stages.append(stage)
    if b_like_a:
        return stages, {d: (zw(-d), [am[d][1].wait_recv, bm[d][1].wait_recv]) for d in dzs}
    return stages + [[pair[1].wait_recv for pair in (*am.values(), *bm.values())]]


def run(stage):
    for step in stage:
        step()


GATHER_COPIES = 31 + 31 + 8 + 8


def attend_kernel(
    kv_ref, q_ref, qseg_ref, aseg_ref, bseg_ref, o_ref,
    a_ref, b_ref, top_ref, total_ref, acc_ref, send_sem, recv_sem, own_sem,
):
    me_seq = lax.axis_index("seq")
    z, x, c = me_seq // (NX * NC), lax.rem(me_seq // NC, NX), lax.rem(me_seq, NC)
    half = kv_ref.shape[0] // 2
    mine = [
        pltpu.make_async_copy(kv_ref.at[pl.ds(0, half)], a_ref.at[z, x, c], own_sem.at[0]),
        pltpu.make_async_copy(kv_ref.at[pl.ds(half, half)], b_ref.at[z, x, c], own_sem.at[1]),
    ]
    for copy in mine:
        copy.start()
    greet([seq_id(z + 1, x, c), seq_id(z - 1, x, c), seq_id(z, x + 1, c), seq_id(z, x - 1, c), seq_id(z, x, 1 - c)])
    for copy in mine:
        copy.wait()
    ring = Ring(send_sem, recv_sem)
    stages, arrivals = torus_gather(
        ring, (z, x, c),
        lambda zz, xx: a_ref.at[zz, xx, c], lambda zz, cc: a_ref.at[zz, :, cc],
        lambda zz, xx: b_ref.at[zz, xx, c], lambda zz, cc: b_ref.at[zz, :, cc], b_like_a=True)

    rows, head = q_ref.shape
    keys = 8 * half
    q = q_ref[...]
    qseg = qseg_ref[...]
    scale = 1.0 / math.sqrt(head)

    def visit(carried, kv, kseg, extra):
        top, total, acc = carried
        s = lax.dot_general(q, kv[:, :head], (((1,), (1,)), ((), ())), preferred_element_type=jnp.float32)
        allowed = kseg == qseg
        if extra is not None:
            allowed = allowed & extra
        s = jnp.where(allowed, s * scale, -1e30)
        new_top = jnp.maximum(top, jnp.max(s, axis=1, keepdims=True))
        w = jnp.exp(s - new_top)
        if extra is not None:
            w = jnp.where(allowed, w, 0.0)
        keep = jnp.exp(top - new_top)
        total = total * keep + jnp.sum(w, axis=1, keepdims=True)
        acc = acc * keep + jnp.dot(w.astype(jnp.bfloat16), kv[:, head:], preferred_element_type=jnp.float32)
        return new_top, total, acc

    def both(zz, state, first):
        flat = lambda ref: ref[zz].reshape(keys, 2 * head)
        causal = (None, None)
        if first:
            row = lax.broadcasted_iota(jnp.int32, (rows, 1), 0) & 127
            qpos = row + lax.rem(me_seq, NX * NC) * 128
            col = lax.broadcasted_iota(jnp.int32, (1, keys), 1)
            kpos = (col >> 6) * 128 + (col & 63)
            causal = (kpos <= qpos, kpos + half <= qpos)
        state = visit(state, flat(a_ref), aseg_ref[zz], causal[0])
        state = visit(state, flat(b_ref), bseg_ref[zz], causal[1])
        top_ref[...], total_ref[...], acc_ref[...] = state

    def look_at(d):
        source, waits = arrivals[d]
        run(waits)
        if d == 0:
            both(source, (
                jnp.full((rows, 1), -1e30, jnp.float32),
                jnp.zeros((rows, 1), jnp.float32),
                jnp.zeros((rows, head), jnp.float32)), True)
        else:
            @pl.when(source < z)
            def _():
                both(source, (top_ref[...], total_ref[...], acc_ref[...]), False)

    for t, stage in enumerate(stages):
        run(stage)
        for d in (0, 1, -1, 2, -2, 3, -3):
            if abs(d) + 3 == t:
                look_at(d)
    look_at(4)
    o_ref[...] = (acc_ref[...] / total_ref[...]).astype(o_ref.dtype)
    ring.finish()


def attend(q, kv, segment_ids, shard, rows):
    half = rows // 2
    halves = segment_ids.reshape(NZ, NX * NC, 2, half)
    aseg = halves[:, :, 0].reshape(NZ, 1, NX * NC * half)
    bseg = halves[:, :, 1].reshape(NZ, 1, NX * NC * half)
    own = lax.dynamic_slice_in_dim(segment_ids, shard * rows, rows, 0)
    qseg = jnp.tile(own, q.shape[0] // rows)[:, None]
    whole = pl.BlockSpec(memory_space=pltpu.VMEM)
    blocks = pltpu.VMEM((NZ, NX, NC, half, kv.shape[1]), kv.dtype)
    count = q.shape[0]
    return pl.pallas_call(
        attend_kernel,
        out_shape=jax.ShapeDtypeStruct(q.shape, jnp.bfloat16),
        in_specs=[whole] * 5,
        out_specs=whole,
        scratch_shapes=[
            blocks, blocks,
            pltpu.VMEM((count, 1), jnp.float32), pltpu.VMEM((count, 1), jnp.float32), pltpu.VMEM(q.shape, jnp.float32),
            pltpu.SemaphoreType.DMA((GATHER_COPIES,)),
            pltpu.SemaphoreType.DMA((GATHER_COPIES,)),
            pltpu.SemaphoreType.DMA((2,)),
        ],
        compiler_params=pltpu.CompilerParams(collective_id=1, has_side_effects=True, vmem_limit_bytes=48 << 20),
        cost_estimate=pl.CostEstimate(flops=2 * 10**9, bytes_accessed=40_000_000, transcendentals=4_000_000),
        name="attend",
    )(kv, q, qseg, aseg, bseg)


CHUNKS, CHUNK = 8, 96
HEAD_START, EVERY = 2, 2
WIDTH = 256
ENC_COPIES = 7 + 7 + 2 * GATHER_COPIES + 8 + 1 + 6
layer_eps = 1e-06
rms_eps = 1e-06
rope_base = 1000000.0


def encoder_kernel(
    start_ref, count_ref, in_ref, out_ref, proj_ref, patches_ref, gain_ref, bin_ref, bout_ref, text_hbm,
    norm_ref, qw_hbm, kw_hbm, vw_hbm, qb_ref, vb_ref, cos_ref, sin_ref,
    q_ref, kv_ref,
    mixed_ref, qkv_ref,
    w_ref, p_ref, select_ref, frame_ref, text_ref, rec_w, rec_p, win, wout, extra, pa, pb, inflow, outflow, passed, vision,
    send_sem, recv_sem, chunk_send, chunk_recv, cast_send, cast_recv, local_sem,
):
    me_seq, section = lax.axis_index("seq"), lax.axis_index("section")
    z, x, c = me_seq // (NX * NC), lax.rem(me_seq // NC, NX), lax.rem(me_seq, NC)
    j = lax.rem(me_seq, NX * NC)
    last = section == 3
    up, down = lax.rem(section + 1, 4), lax.rem(section + 3, 4)
    shards = NZ * NX * NC
    ahead, behind = lax.rem(me_seq + 1, shards), lax.rem(me_seq + shards - 1, shards)
    others = [lax.rem(j + k, 8) for k in range(8)]
    sources = [lax.rem(j + 8 - k, 8) for k in range(8)]
    member = lambda k: z * (NX * NC) + k

    frame = pltpu.make_async_copy(patches_ref, frame_ref, local_sem.at[2])
    text = pltpu.make_async_copy(text_hbm, text_ref, local_sem.at[11])
    heads = qw_hbm.shape[1]
    head = kw_hbm.shape[1]
    loads = [text] + [
        pltpu.make_async_copy(ref, qkv_ref.at[:, pl.ds(at, ref.shape[1])], local_sem.at[12 + n])
        for n, (ref, at) in enumerate(((qw_hbm, 0), (kw_hbm, heads), (vw_hbm, heads + head)))
    ]
    for copy in loads:
        copy.start()

    @pl.when(section == 0)
    def _():
        frame.start()

    depth = in_ref.shape[0]
    w_ref[:, 16:, :] = jnp.zeros((8, 16, w_ref.shape[2]), w_ref.dtype)
    p_ref[:, 16:, :] = jnp.zeros((8, 16, p_ref.shape[2]), p_ref.dtype)
    p_ref[7] = jnp.zeros(p_ref.shape[1:], p_ref.dtype)
    for k in range(8):
        w_ref[k, :depth, :256] = in_ref[:, 256 * k : 256 * k + 256]
        w_ref[k, :depth, 256:512] = out_ref[:, 256 * k : 256 * k + 256]
        w_ref[k, :depth, 512:] = (out_ref if k % 2 else in_ref)[:, 2048:]
        if k < 7:
            p_ref[k, :depth] = proj_ref[:, 512 * k : 512 * k + 512]
    own = [
        pltpu.make_async_copy(w_ref.at[j], rec_w.at[j], local_sem.at[0]),
        pltpu.make_async_copy(p_ref.at[j], rec_p.at[j], local_sem.at[1]),
    ]
    rows = win.shape[3]
    at = lax.broadcasted_iota(jnp.int32, (rows, 256), 0)
    slot = lax.broadcasted_iota(jnp.int32, (rows, 256), 1)
    inner = slot & 31
    pick = jnp.where((inner < depth) & (at == depth * (slot >> 5) + inner), 1.0, 0.0).astype(jnp.bfloat16)

    greet(
        [member(k) for k in others[1:]]
        + [seq_id(z + 1, x, c), seq_id(z - 1, x, c), ahead, behind, {"section": up}, {"section": down}]
    )
    ring = Ring(send_sem, recv_sem)
    spread_w = [ring.copy(w_ref.at[others[k]], rec_w.at[sources[k]], member(others[k]), rec_w.at[j]) for k in range(1, 8)]
    spread_p = [ring.copy(p_ref.at[others[k]], rec_p.at[sources[k]], member(others[k]), rec_p.at[j]) for k in range(1, 8)]
    for out, _ in spread_w:
        out.start()
    for copy in own:
        copy.start()
    for copy in own:
        copy.wait()
    for _, into in spread_w:
        into.wait_recv()
    block = jnp.dot(pick, rec_w[...].reshape(-1, rec_w.shape[2]), preferred_element_type=jnp.float32)
    block = block.astype(jnp.bfloat16)
    wout[x, c, z] = block[:, 256:512]
    win[x, c, z] = block[:, :256]
    extra[c, z] = block[:, 512:]

    def views(a, b):
        return (
            lambda zz, xx: a.at[xx, c, zz], lambda zz, cc: a.at[:, cc, zz],
            lambda zz, xx: b.at[xx, c, zz], lambda xx, cc: b.at[xx, cc])

    stages = torus_gather(ring, (z, x, c), *views(win, wout))
    s = 1 - 2 * c
    zw = lambda k: lax.rem(z + k + 2 * NZ, NZ)
    zm, zo = seq_id(z + s, x, c), seq_id(z - s, x, c)
    ez_m = [ring.copy(extra.at[c, zw(-k * s)], extra.at[c, zw(-(k + 1) * s)], zm) for k in range(4)]
    ez_o = [ring.copy(extra.at[c, zw(k * s)], extra.at[c, zw((k + 1) * s)], zo) for k in range(3)]
    e_mate = ring.copy(extra.at[c], extra.at[1 - c], seq_id(z, x, 1 - c))
    for n, stage in enumerate(stages):
        if n == 7:
            e_mate[0].start()
        run(stage)
        if n == 2:
            ez_m[0][0].start()
            ez_o[0][0].start()
        if 3 <= n < 7:
            ez_m[n - 3][1].wait_recv()
            if n < 6:
                ez_m[n - 2][0].start()
                ez_o[n - 3][1].wait_recv()
            if n < 5:
                ez_o[n - 2][0].start()
    e_mate[1].wait_recv()
    for out, _ in spread_p:
        out.start()

    def lay_out_p():
        for _, into in spread_p:
            into.wait_recv()
        block = jnp.dot(pick, rec_p[...].reshape(-1, rec_p.shape[2]), preferred_element_type=jnp.float32)
        block = block.astype(jnp.bfloat16)
        pa[x, c, z] = block[:, :256]
        pb[x, c, z] = block[:, 256:]

    p_stages = [[lay_out_p]] + torus_gather(ring, (z, x, c), *views(pa, pb))

    @pl.when(section == 0)
    def _():
        frame.wait()
        full = frame_ref.shape[0] // CHUNK
        for i in range(full):
            inflow[i] = frame_ref[CHUNK * i : CHUNK * i + CHUNK]
        inflow[full] = jnp.zeros((CHUNK, frame_ref.shape[1]), inflow.dtype)
        inflow[full, : frame_ref.shape[0] - CHUNK * full] = frame_ref[CHUNK * full :]

    for n in range(3 * HEAD_START):
        @pl.when(n < HEAD_START * section)
        def _():
            run(p_stages[n])

    count = text_ref.shape[0]
    first, kept = start_ref[me_seq], count_ref[me_seq]

    @pl.when(last)
    def _():
        shape = select_ref.shape
        token = lax.broadcasted_iota(jnp.int32, (shape[0], 1), 0) + (me_seq * count - first)
        patch = lax.broadcasted_iota(jnp.int32, (1, shape[1]), 1)
        down = (patch * 607) >> 14
        across = patch - 27 * down
        cell = jnp.where(patch < 729, (down >> 1) * 14 + (across >> 1), -1)
        share = jnp.where(down == 26, 1.0, 0.5) * jnp.where(across == 26, 1.0, 0.5)
        token = jnp.where((token >= 0) & (token < kept), token, -2)
        select_ref[...] = jnp.where(token == cell, share, 0.0).astype(jnp.bfloat16)

    def chunk_copy(i):
        return pltpu.make_async_remote_copy(
            src_ref=outflow.at[i], dst_ref=inflow.at[i], send_sem=chunk_send.at[i], recv_sem=chunk_recv.at[i],
            device_id={"section": up}, device_id_type=pl.DeviceIdType.MESH)

    def one_chunk(i, nothing):
        @pl.when(section > 0)
        def _():
            chunk_copy(i).wait_recv()

        widened = inflow[i].astype(jnp.float32)
        center = widened - jnp.mean(widened, axis=1, keepdims=True)
        spread = jnp.mean(center * center, axis=1, keepdims=True)
        normed = (center * lax.rsqrt(spread + layer_eps) * gain_ref[...]).astype(jnp.bfloat16)

        def hidden(w_in, b_in):
            v = jnp.dot(normed, w_in, preferred_element_type=jnp.float32) + b_in
            return jax.nn.gelu(v, approximate=True).astype(jnp.bfloat16)

        flat = lambda ref, k: ref[k // 2, k % 2].reshape(8 * rows, 256)
        parts = [hidden(flat(win, k), bin_ref[:, 256 * k : 256 * k + 256]) for k in range(8)]
        parts.append(hidden(extra[0].reshape(8 * rows, 128), bin_ref[:, 2048:]))
        for at in range(0, 8 * rows, WIDTH):
            to = min(at + WIDTH, 8 * rows)
            out = widened[:, at:to] + bout_ref[:, at:to]
            for k in range(9):
                w_out = flat(wout, k) if k < 8 else extra[1].reshape(8 * rows, 128)
                out += lax.dot_general(
                    parts[k], w_out[at:to], (((1,), (1,)), ((), ())), preferred_element_type=jnp.float32)
            outflow[i, :, at:to] = out.astype(jnp.bfloat16)

        @pl.when(jnp.logical_not(last))
        def _():
            chunk_copy(i).start()

        for n, stage in enumerate(p_stages):
            @pl.when((i == EVERY * (n - HEAD_START * section)) & (section > 0))
            def _():
                run(stage)

        return nothing

    lax.fori_loop(0, CHUNKS, one_chunk, 0)

    for n, stage in enumerate(p_stages):
        @pl.when((EVERY * (n - HEAD_START * section) >= CHUNKS) | (section == 0))
        def _():
            run(stage)

    @pl.when(jnp.logical_not(last))
    def _():
        for i in range(CHUNKS):
            chunk_copy(i).wait_send()

    over = pltpu.make_async_remote_copy(
        src_ref=passed.at[0], dst_ref=passed.at[1], send_sem=local_sem.at[3], recv_sem=local_sem.at[4],
        device_id={"seq": ahead}, device_id_type=pl.DeviceIdType.MESH)
    parts = vision.shape[0]
    cast = lambda h, n, to: pltpu.make_async_remote_copy(
        src_ref=vision.at[h], dst_ref=vision.at[h], send_sem=cast_send.at[n], recv_sem=cast_recv.at[h],
        device_id={"section": to}, device_id_type=pl.DeviceIdType.MESH)

    @pl.when(last)
    def _():
        encoded = outflow[...].reshape(CHUNKS * CHUNK, outflow.shape[2])
        passed[0] = jnp.dot(select_ref[count:], encoded, preferred_element_type=jnp.float32).astype(jnp.bfloat16)
        over.start()
        mine = jnp.dot(select_ref[:count], encoded, preferred_element_type=jnp.float32)
        over.wait()
        mine = mine + jnp.where(me_seq > 0, passed[1].astype(jnp.float32), 0.0)
        vision[...] = mine.astype(jnp.bfloat16).reshape(vision.shape)
        copies = []
        for h in range(parts):
            copies += [cast(h, h, 0), cast(parts - 1 - h, parts + h, 2)]
        for copy in copies:
            copy.start()
        for copy in copies:
            copy.wait_send()

    for me, order in ((0, range(parts)), (2, range(parts - 1, -1, -1))):
        @pl.when(section == me)
        def _():
            for h in list(order)[: parts // 2]:
                cast(h, h, 1).wait_recv()
                cast(h, h, 1).start()
            for h in list(order)[parts // 2 :]:
                cast(h, h, 1).wait_recv()
            for h in list(order)[: parts // 2]:
                cast(h, h, 1).wait_send()

    @pl.when(section == 1)
    def _():
        for h in range(parts):
            cast(h, h, 1).wait_recv()

    tokens = vision[...].reshape(count, vision.shape[2])
    for copy in loads:
        copy.wait()
    slots = lax.broadcasted_iota(jnp.int32, (count, 1), 0) + me_seq * count
    before = jnp.maximum(me_seq - 1, 0)
    prior = slots - start_ref[before]
    valid = (slots >= first) & (slots < first + kept)
    valid = valid | ((me_seq > 0) & (prior >= 0) & (prior < count_ref[before]))
    squares = jnp.zeros((count, 1), jnp.float32)
    for k in range(7):
        for n, ref in enumerate((pa, pb)):
            out = jnp.dot(tokens, ref[k // 2, k % 2].reshape(8 * rows, 256), preferred_element_type=jnp.float32)
            at = 512 * k + 256 * n
            out = jnp.where(valid, out.astype(jnp.bfloat16), text_ref[:, at : at + 256])
            mixed_ref[:, at : at + 256] = out
            out = out.astype(jnp.float32)
            squares += jnp.sum(out * out, axis=1, keepdims=True)
    factor = lax.rsqrt(squares / mixed_ref.shape[1] + rms_eps)
    normed = (mixed_ref[...].astype(jnp.float32) * factor * norm_ref[...]).astype(jnp.bfloat16)
    rope = lambda u: u * cos_ref[...] + pltpu.roll(u, head // 2, 1) * sin_ref[...]
    for n in range(0, heads, 2 * head):
        two = jnp.dot(normed, qkv_ref[:, n : n + 2 * head], preferred_element_type=jnp.float32)
        two = two + qb_ref[:, n : n + 2 * head]
        for i in range(2):
            at = (n // head + i) * count
            q_ref[at : at + count] = rope(two[:, i * head : (i + 1) * head]).astype(jnp.bfloat16)
    two = jnp.dot(normed, qkv_ref[:, heads:], preferred_element_type=jnp.float32)
    kv_ref[:, :head] = rope(two[:, :head]).astype(jnp.bfloat16)
    kv_ref[:, head:] = (two[:, head:] + vb_ref[...]).astype(jnp.bfloat16)
    ring.finish()


def encode(start, kept, w_in, w_out, proj, patches, gain, b_in, b_out, text, norm, qw, kw, vw, qb, vb, cos, sin):
    rows, width = 8 * w_in.shape[0], patches.shape[1]
    whole = pl.BlockSpec(memory_space=pltpu.VMEM)
    scalars = pl.BlockSpec(memory_space=pltpu.SMEM)
    away = pl.BlockSpec(memory_space=pl.ANY)
    bf = jnp.bfloat16
    big = pltpu.VMEM((NX, NC, NZ, rows, 256), bf)
    spread = [pltpu.VMEM((8, 32, 640), bf), pltpu.VMEM((8, 32, 512), bf)]
    return pl.pallas_call(
        encoder_kernel,
        out_shape=(
            jax.ShapeDtypeStruct((text.shape[0] * (qw.shape[1] // kw.shape[1]), kw.shape[1]), bf),
            jax.ShapeDtypeStruct((text.shape[0], 2 * kw.shape[1]), bf),
        ),
        in_specs=[scalars, scalars, whole, whole, whole, away, whole, whole, whole, away]
        + [whole, away, away, away] + [whole] * 4,
        out_specs=(whole, whole),
        scratch_shapes=[
            pltpu.VMEM(text.shape, bf), pltpu.VMEM((text.shape[1], qw.shape[1] + 2 * kw.shape[1]), bf),
            *spread, pltpu.VMEM((2 * text.shape[0], CHUNKS * CHUNK), bf),
            pltpu.VMEM(patches.shape, bf), pltpu.VMEM(text.shape, bf), *spread,
            big, big, pltpu.VMEM((NC, NZ, rows, 128), bf), big, big,
            pltpu.VMEM((CHUNKS, CHUNK, width), bf), pltpu.VMEM((CHUNKS, CHUNK, width), bf),
            pltpu.VMEM((2, text.shape[0], width), bf), pltpu.VMEM((4, text.shape[0] // 4, width), bf),
            pltpu.SemaphoreType.DMA((ENC_COPIES,)), pltpu.SemaphoreType.DMA((ENC_COPIES,)),
            pltpu.SemaphoreType.DMA((CHUNKS,)), pltpu.SemaphoreType.DMA((CHUNKS,)),
            pltpu.SemaphoreType.DMA((8,)), pltpu.SemaphoreType.DMA((4,)),
            pltpu.SemaphoreType.DMA((16,)),
        ],
        compiler_params=pltpu.CompilerParams(collective_id=0, has_side_effects=True, vmem_limit_bytes=60 << 20),
        cost_estimate=pl.CostEstimate(flops=10**10, bytes_accessed=40_000_000, transcendentals=2_000_000),
        name="encode",
    )(start, kept, w_in, w_out, proj, patches, gain, b_in, b_out, text, norm, qw, kw, vw, qb, vb, cos, sin)


def per_device(
    patches,
    fc_gain,
    fc_in,
    fc_in_bias,
    fc_out,
    fc_out_bias,
    proj_weight,
    text_embed,
    frame_start,
    frame_count,
    segment_ids,
    norm_gain,
    query_weight,
    query_bias,
    key_weight,
    value_weight,
    value_bias,
):
    shard_id = lax.axis_index("seq")
    shard_rows = text_embed.shape[0]
    head_size = key_weight.shape[1]
    group_size = query_weight.shape[1] // head_size

    local_slots = jnp.arange(shard_rows, dtype=jnp.int32)
    positions = shard_id * shard_rows + local_slots
    half_dim = head_size // 2
    inv_rates = jnp.exp(
        jnp.arange(half_dim, dtype=jnp.float32) * (-2.0 * math.log(rope_base) / head_size)
    )
    angles = positions.astype(jnp.float32)[:, None] * inv_rates[None, :]
    cosine, sine = jnp.cos(angles), jnp.sin(angles)
    queries, stacked = encode(
        frame_start, frame_count, fc_in[0], fc_out[0].T, proj_weight, patches[0],
        fc_gain, fc_in_bias, fc_out_bias, text_embed,
        norm_gain[None], query_weight, key_weight, value_weight, query_bias[None], value_bias[None],
        jnp.concatenate([cosine, cosine], axis=1), jnp.concatenate([-sine, sine], axis=1),
    )
    attended = attend(queries, stacked, segment_ids, shard_id, shard_rows)
    attended = attended.reshape(group_size, shard_rows, head_size).transpose(1, 0, 2)
    return attended.reshape(shard_rows, group_size * head_size)


def solution(mesh):
    return jax.shard_map(
        per_device,
        mesh=mesh,
        in_specs=(
            P("seq", None, None),
            P("section", None),
            P("section", "seq", None),
            P("section", None),
            P("section", None, "seq"),
            P("section", None),
            P("seq", None),
            P("seq", None),
            P(),
            P(),
            P(),
            P(),
            P(None, "section"),
            P("section"),
            P(None, "section"),
            P(None, "section"),
            P("section"),
        ),
        out_specs=P("seq", "section"),
        check_vma=False,
    )
```

time: 216 us -> 180 us (0.83)
  Pallas kernels: 191 us -> 173 us
  other arithmetic: 10.3 us -> 1.08 us
  local copies, waits for them, and re-layouts: 10.3 us -> 5.85 us
  matrix products: 2.99 us -> 0 us
    pallas_call x3 -> x2, Pallas kernels: 191 us -> 173 us  [the longest x1 135 us: encode(): pl.pallas_call(encoder_kernel, out_shape=(jax.ShapeDtypeStruct((text.shap...]
    convert_element_type x4 -> x1, other arithmetic: 4.14 us -> 0.01 us  [per_device(): angles = positions.astype(jnp.float32)[:, None] * inv_rates[None, :]]
    dot_general x3 -> x0, matrix products: 2.99 us -> none  [the longest x1 1.8 us: per_device(): jnp.dot(normed, value_weight, preferred_element_type=jnp.float32)]
    slice x5 -> x1, local copies, waits for them, and re-layouts: 2.37 us -> 0.18 us  [attend(): bseg = halves[:, :, 1].reshape(NZ, 1, NX * NC * half)]
where the time goes in v3:
time: 180 us
  Pallas kernels  173 us (96%)
  local copies, waits for them, and re-layouts  5.85 us (3%)
    pallas_call x1, Pallas kernels, encode(): pl.pallas_call(encoder_kernel, out_shape=(jax.ShapeDtypeStruct((text.shap...  135 us
    pallas_call x1, Pallas kernels, attend(): pl.pallas_call(attend_kernel, out_shape=jax.ShapeDtypeStruct(q.shape, jnp...  38.4 us

profile of v3, /device:TPU:232, one launch (start us, length us, event | category | flops | bytes accessed | tf_op | source)
XLA Modules:
  0.0 180.1 jit_solution(8143223321735754228)
XLA Ops:
  0.0 0.8 dynamic_slice.3
  0.8 1.3 broadcast_in_dim.11.norm_ref
  2.1 0.9 reshape.20
  3.0 0.2 slice_reduce_fusion
  3.2 0.1 reshape_squeeze.7.bseg_ref
  3.2 0.1 reshape_squeeze.6.aseg_ref
  3.3 0.3 fusion
  3.7 0.8 pad_maximum_fusion
  4.4 134.7 %encode.1 = (bf16[512,128]{1,0:T(8,128)(2,1)}, bf16[128,256]{1,0:T(8,128)(2,1)}) custom-call(s32[64]{0:T(128)} %start_ref.1, s32[64]{0:T(128)} %count_ref.1, bf16[18,2176]{1,0:T(8,128)(2,1)} %bitcast.18, bf16[18,2176]{1,0:T(8,128)(2,1)} %bitcast.19, bf16[18,3584]{1,0:T(8,128)(2,1)} %proj_ref.1, bf16[729,1152]{1,0:T(8,128)(2,1)} %bitcast.17, ...), custom_call_target="tpu_custom_call" | custom-call | flops 10000000000 | bytes 40000000 | tf_op jit(solution)/shard_map/encode/pallas_call | solution.py:494
  139.1 0.1 copy.19.qseg_ref
  139.3 0.0 copy-start
  139.3 0.9 copy-done
  140.2 0.0 copy-start.1
  140.2 0.8 copy-done.1
  141.0 38.4 %attend.1 = bf16[512,128]{1,0:T(8,128)(2,1)S(1)} custom-call(bf16[128,256]{1,0:T(8,128)(2,1)S(1)} %copy-done.1, bf16[512,128]{1,0:T(8,128)(2,1)S(1)} %copy-done, s32[512,1]{1,0:T(8,128)S(1)} %copy.19.qseg_ref, s32[8,1,512]{2,1,0:T(1,128)S(1)} %reshape_squeeze.6.aseg_ref, s32[8,1,512]{2,1,0:T(1,128)S(1)} %reshape_squeeze.7.bseg_ref), custom_call_target="tpu_custom_call" | custom-call | flops 2000000000 | bytes 40000000 | tf_op jit(solution)/shard_map/attend/pallas_call | solution.py:188
  179.5 0.7 copy.23
  (3 shorter events, 0.0 us)
Async XLA Ops:
  139.3 0.9 copy-start
  140.2 0.8 copy-start.1

commit v4 on v3

--- a/solution.py
+++ b/solution.py
@@ -66,8 +66,8 @@
             continue
         source = (dx, toward(dz)) if along_z else (toward(dx), dz)
         target = (zm if dz > 0 else zo) if along_z else (xm if dx > 0 else xo)
-        copies[key] = ring.copy(one[kind](*source), one[kind](dx, dz), target)
-        after[(kind, *source)].append(copies[key])
+        copies[key] = [ring.copy(sent, got, target) for sent, got in zip(one[kind](*source), one[kind](dx, dz))]
+        after[(kind, *source)] += copies[key]
     am = {d: ring.copy(a_many(zw(d), c), a_many(zw(-d), 1 - c), mate) for d in dzs}
     bw, bds, late = (zw, dzs, 2) if b_like_a else (xw, dxs, 4)
     bm = {d: ring.copy(b_many(bw(d), c), b_many(bw(-d), 1 - c), mate) for d in bds}
@@ -77,7 +77,7 @@
         for key in keys:
             if abs(key[1]) + abs(key[2]) == t:
                 if t:
-                    stage.append(copies[key][1].wait_recv)
+                    stage += [into.wait_recv for _, into in copies[key]]
                 stage += [out.start for out, _ in after[key]]
         stage += [am[d][0].start for d in dzs if abs(d) + 2 == t]
         stage += [bm[d][0].start for d in bds if abs(d) + late == t]
@@ -96,8 +96,8 @@
 
 
 def attend_kernel(
-    kv_ref, q_ref, qseg_ref, aseg_ref, bseg_ref, o_ref,
-    a_ref, b_ref, top_ref, total_ref, acc_ref, send_sem, recv_sem, own_sem,
+    kv_ref, q_hbm, qseg_ref, kseg_ref, o_ref,
+    q_ref, a_ref, b_ref, top_ref, total_ref, acc_ref, send_sem, recv_sem, own_sem,
 ):
     me_seq = lax.axis_index("seq")
     z, x, c = me_seq // (NX * NC), lax.rem(me_seq // NC, NX), lax.rem(me_seq, NC)
@@ -108,78 +108,80 @@
     ]
     for copy in mine:
         copy.start()
+    queries = pltpu.make_async_copy(q_hbm, q_ref, own_sem.at[2])
+    queries.start()
     greet([seq_id(z + 1, x, c), seq_id(z - 1, x, c), seq_id(z, x + 1, c), seq_id(z, x - 1, c), seq_id(z, x, 1 - c)])
     for copy in mine:
         copy.wait()
     ring = Ring(send_sem, recv_sem)
     stages, arrivals = torus_gather(
         ring, (z, x, c),
-        lambda zz, xx: a_ref.at[zz, xx, c], lambda zz, cc: a_ref.at[zz, :, cc],
-        lambda zz, xx: b_ref.at[zz, xx, c], lambda zz, cc: b_ref.at[zz, :, cc], b_like_a=True)
+        lambda zz, xx: (a_ref.at[zz, xx, c],), lambda zz, cc: a_ref.at[zz, :, cc],
+        lambda zz, xx: (b_ref.at[zz, xx, c],), lambda zz, cc: b_ref.at[zz, :, cc], b_like_a=True)
 
     rows, head = q_ref.shape
-    keys = 8 * half
+    queries.wait()
     q = q_ref[...]
     qseg = qseg_ref[...]
-    scale = 1.0 / math.sqrt(head)
-
-    def visit(carried, kv, kseg, extra):
-        top, total, acc = carried
-        s = lax.dot_general(q, kv[:, :head], (((1,), (1,)), ((), ())), preferred_element_type=jnp.float32)
-        allowed = kseg == qseg
-        if extra is not None:
-            allowed = allowed & extra
-        s = jnp.where(allowed, s * scale, -1e30)
-        new_top = jnp.maximum(top, jnp.max(s, axis=1, keepdims=True))
-        w = jnp.exp(s - new_top)
-        if extra is not None:
-            w = jnp.where(allowed, w, 0.0)
-        keep = jnp.exp(top - new_top)
-        total = total * keep + jnp.sum(w, axis=1, keepdims=True)
-        acc = acc * keep + jnp.dot(w.astype(jnp.bfloat16), kv[:, head:], preferred_element_type=jnp.float32)
-        return new_top, total, acc
-
-    def both(zz, state, first):
-        flat = lambda ref: ref[zz].reshape(keys, 2 * head)
-        causal = (None, None)
+    scale = math.log2(math.e) / math.sqrt(head)
+
+    def visit(zz, cc, first):
+        kv = [ref[zz, :, cc].reshape(NX * half, 2 * head) for ref in (a_ref, b_ref)]
+        allowed = [kseg_ref[zz, cc, n : n + 1] == qseg for n in range(2)]
         if first:
             row = lax.broadcasted_iota(jnp.int32, (rows, 1), 0) & 127
             qpos = row + lax.rem(me_seq, NX * NC) * 128
-            col = lax.broadcasted_iota(jnp.int32, (1, keys), 1)
-            kpos = (col >> 6) * 128 + (col & 63)
-            causal = (kpos <= qpos, kpos + half <= qpos)
-        state = visit(state, flat(a_ref), aseg_ref[zz], causal[0])
-        state = visit(state, flat(b_ref), bseg_ref[zz], causal[1])
-        top_ref[...], total_ref[...], acc_ref[...] = state
-
-    def look_at(d):
+            col = lax.broadcasted_iota(jnp.int32, (1, NX * half), 1)
+            kpos = (col >> 6) * 256 + cc * 128 + (col & 63)
+            allowed = [ok & (kpos + n * half <= qpos) for n, ok in enumerate(allowed)]
+        scores = [
+            lax.dot_general(q, one[:, :head], (((1,), (1,)), ((), ())), preferred_element_type=jnp.float32)
+            for one in kv
+        ]
+        scores = [jnp.where(ok, s * scale, -1e30) for s, ok in zip(scores, allowed)]
+        top = jnp.max(jnp.maximum(*scores), axis=1, keepdims=True)
+        if not (first and cc is c):
+            top = jnp.maximum(top_ref[...], top)
+        weights = [jnp.exp2(s - top) for s in scores]
+        total = jnp.sum(weights[0] + weights[1], axis=1, keepdims=True)
+        acc = sum(
+            jnp.dot(w.astype(jnp.bfloat16), one[:, head:], preferred_element_type=jnp.float32)
+            for w, one in zip(weights, kv))
+        if not (first and cc is c):
+            keep = jnp.exp2(top_ref[...] - top)
+            total += total_ref[...] * keep
+            acc += acc_ref[...] * keep
+        top_ref[...], total_ref[...], acc_ref[...] = top, total, acc
+
+    def look_at(d, cc):
         source, waits = arrivals[d]
-        run(waits)
+        if cc is not c:
+            run(waits)
         if d == 0:
-            both(source, (
-                jnp.full((rows, 1), -1e30, jnp.float32),
-                jnp.zeros((rows, 1), jnp.float32),
-                jnp.zeros((rows, head), jnp.float32)), True)
+            visit(source, cc, True)
         else:
             @pl.when(source < z)
             def _():
-                both(source, (top_ref[...], total_ref[...], acc_ref[...]), False)
-
+                visit(source, cc, False)
+
+    other = 1 - c
+    ds = (0, 1, -1, 2, -2, 3, -3, 4)
     for t, stage in enumerate(stages):
         run(stage)
-        for d in (0, 1, -1, 2, -2, 3, -3):
+        for d in ds:
             if abs(d) + 3 == t:
-                look_at(d)
-    look_at(4)
+                look_at(d, other)
+        for d in ds:
+            if abs(d) + 2 == t:
+                look_at(-d if d != 4 else 4, c)
+    look_at(4, other)
     o_ref[...] = (acc_ref[...] / total_ref[...]).astype(o_ref.dtype)
     ring.finish()
 
 
 def attend(q, kv, segment_ids, shard, rows):
     half = rows // 2
-    halves = segment_ids.reshape(NZ, NX * NC, 2, half)
-    aseg = halves[:, :, 0].reshape(NZ, 1, NX * NC * half)
-    bseg = halves[:, :, 1].reshape(NZ, 1, NX * NC * half)
+    kseg = segment_ids.reshape(NZ, NX, NC, 2, half).transpose(0, 2, 3, 1, 4).reshape(NZ, NC, 2, NX * half)
     own = lax.dynamic_slice_in_dim(segment_ids, shard * rows, rows, 0)
     qseg = jnp.tile(own, q.shape[0] // rows)[:, None]
     whole = pl.BlockSpec(memory_space=pltpu.VMEM)
@@ -188,25 +190,26 @@
     return pl.pallas_call(
         attend_kernel,
         out_shape=jax.ShapeDtypeStruct(q.shape, jnp.bfloat16),
-        in_specs=[whole] * 5,
+        in_specs=[pl.BlockSpec(memory_space=pl.ANY)] * 2 + [whole] * 2,
         out_specs=whole,
         scratch_shapes=[
-            blocks, blocks,
+            pltpu.VMEM(q.shape, q.dtype), blocks, blocks,
             pltpu.VMEM((count, 1), jnp.float32), pltpu.VMEM((count, 1), jnp.float32), pltpu.VMEM(q.shape, jnp.float32),
             pltpu.SemaphoreType.DMA((GATHER_COPIES,)),
             pltpu.SemaphoreType.DMA((GATHER_COPIES,)),
-            pltpu.SemaphoreType.DMA((2,)),
+            pltpu.SemaphoreType.DMA((3,)),
         ],
         compiler_params=pltpu.CompilerParams(collective_id=1, has_side_effects=True, vmem_limit_bytes=48 << 20),
         cost_estimate=pl.CostEstimate(flops=2 * 10**9, bytes_accessed=40_000_000, transcendentals=4_000_000),
         name="attend",
-    )(kv, q, qseg, aseg, bseg)
+    )(kv, q, qseg, kseg)
 
 
 CHUNKS, CHUNK = 8, 96
 HEAD_START, EVERY = 2, 2
-WIDTH = 256
-ENC_COPIES = 7 + 7 + 2 * GATHER_COPIES + 8 + 1 + 6
+WIDTH = 1152
+SPLIT = 112
+ENC_COPIES = 14 + 2 * (3 * 31 + 12) + 8
 layer_eps = 1e-06
 rms_eps = 1e-06
 rope_base = 1000000.0
@@ -218,7 +221,7 @@
     q_ref, kv_ref,
     mixed_ref, qkv_ref,
     w_ref, p_ref, select_ref, frame_ref, text_ref, rec_w, rec_p, win, wout, extra, pa, pb, inflow, outflow, passed, vision,
-    send_sem, recv_sem, chunk_send, chunk_recv, cast_send, cast_recv, local_sem,
+    send_sem, recv_sem, chunk_send, chunk_recv, cast_send, cast_recv, over_send, over_recv, local_sem,
 ):
     me_seq, section = lax.axis_index("seq"), lax.axis_index("section")
     z, x, c = me_seq // (NX * NC), lax.rem(me_seq // NC, NX), lax.rem(me_seq, NC)
@@ -289,8 +292,10 @@
 
     def views(a, b):
         return (
-            lambda zz, xx: a.at[xx, c, zz], lambda zz, cc: a.at[:, cc, zz],
-            lambda zz, xx: b.at[xx, c, zz], lambda xx, cc: b.at[xx, cc])
+            lambda zz, xx: (a.at[xx, c, zz, pl.ds(0, SPLIT)],),
+            lambda zz, cc: a.at[:, cc, zz],
+            lambda zz, xx: (b.at[xx, c, zz], a.at[xx, c, zz, pl.ds(SPLIT, rows - SPLIT)]),
+            lambda xx, cc: b.at[xx, cc])
 
     stages = torus_gather(ring, (z, x, c), *views(win, wout))
     s = 1 - 2 * c
@@ -356,15 +361,20 @@
         token = jnp.where((token >= 0) & (token < kept), token, -2)
         select_ref[...] = jnp.where(token == cell, share, 0.0).astype(jnp.bfloat16)
 
-    def chunk_copy(i):
+    columns = [(at, min(WIDTH, 8 * rows - at)) for at in range(0, 8 * rows, WIDTH)]
+
+    def chunk_copy(i, n):
+        at, size = columns[n]
         return pltpu.make_async_remote_copy(
-            src_ref=outflow.at[i], dst_ref=inflow.at[i], send_sem=chunk_send.at[i], recv_sem=chunk_recv.at[i],
+            src_ref=outflow.at[i, :, pl.ds(at, size)], dst_ref=inflow.at[i, :, pl.ds(at, size)],
+            send_sem=chunk_send.at[i, n], recv_sem=chunk_recv.at[i, n],
             device_id={"section": up}, device_id_type=pl.DeviceIdType.MESH)
 
     def one_chunk(i, nothing):
         @pl.when(section > 0)
         def _():
-            chunk_copy(i).wait_recv()
+            for n in range(len(columns)):
+                chunk_copy(i, n).wait_recv()
 
         widened = inflow[i].astype(jnp.float32)
         center = widened - jnp.mean(widened, axis=1, keepdims=True)
@@ -378,8 +388,8 @@
         flat = lambda ref, k: ref[k // 2, k % 2].reshape(8 * rows, 256)
         parts = [hidden(flat(win, k), bin_ref[:, 256 * k : 256 * k + 256]) for k in range(8)]
         parts.append(hidden(extra[0].reshape(8 * rows, 128), bin_ref[:, 2048:]))
-        for at in range(0, 8 * rows, WIDTH):
-            to = min(at + WIDTH, 8 * rows)
+        for n, (at, size) in enumerate(columns):
+            to = at + size
             out = widened[:, at:to] + bout_ref[:, at:to]
             for k in range(9):
                 w_out = flat(wout, k) if k < 8 else extra[1].reshape(8 * rows, 128)
@@ -387,9 +397,9 @@
                     parts[k], w_out[at:to], (((1,), (1,)), ((), ())), preferred_element_type=jnp.float32)
             outflow[i, :, at:to] = out.astype(jnp.bfloat16)
 
-        @pl.when(jnp.logical_not(last))
-        def _():
-            chunk_copy(i).start()
+            @pl.when(jnp.logical_not(last))
+            def _():
+                chunk_copy(i, n).start()
 
         for n, stage in enumerate(p_stages):
             @pl.when((i == EVERY * (n - HEAD_START * section)) & (section > 0))
@@ -408,12 +418,14 @@
     @pl.when(jnp.logical_not(last))
     def _():
         for i in range(CHUNKS):
-            chunk_copy(i).wait_send()
-
-    over = pltpu.make_async_remote_copy(
-        src_ref=passed.at[0], dst_ref=passed.at[1], send_sem=local_sem.at[3], recv_sem=local_sem.at[4],
+            for n in range(len(columns)):
+                chunk_copy(i, n).wait_send()
+
+    over = lambda h: pltpu.make_async_remote_copy(
+        src_ref=passed.at[0, h], dst_ref=passed.at[1, h], send_sem=over_send.at[h], recv_sem=over_recv.at[h],
         device_id={"seq": ahead}, device_id_type=pl.DeviceIdType.MESH)
     parts = vision.shape[0]
+    order, handed = (0, 3, 1, 2), {0: (0, 1), 2: (3, 2)}
     cast = lambda h, n, to: pltpu.make_async_remote_copy(
         src_ref=vision.at[h], dst_ref=vision.at[h], send_sem=cast_send.at[n], recv_sem=cast_recv.at[h],
         device_id={"section": to}, device_id_type=pl.DeviceIdType.MESH)
@@ -421,29 +433,31 @@
     @pl.when(last)
     def _():
         encoded = outflow[...].reshape(CHUNKS * CHUNK, outflow.shape[2])
-        passed[0] = jnp.dot(select_ref[count:], encoded, preferred_element_type=jnp.float32).astype(jnp.bfloat16)
-        over.start()
+        out = jnp.dot(select_ref[count:], encoded, preferred_element_type=jnp.float32)
+        passed[0] = out.astype(jnp.bfloat16).reshape(vision.shape)
+        for h in order:
+            over(h).start()
         mine = jnp.dot(select_ref[:count], encoded, preferred_element_type=jnp.float32)
-        over.wait()
-        mine = mine + jnp.where(me_seq > 0, passed[1].astype(jnp.float32), 0.0)
-        vision[...] = mine.astype(jnp.bfloat16).reshape(vision.shape)
-        copies = []
-        for h in range(parts):
-            copies += [cast(h, h, 0), cast(parts - 1 - h, parts + h, 2)]
-        for copy in copies:
-            copy.start()
-        for copy in copies:
-            copy.wait_send()
-
-    for me, order in ((0, range(parts)), (2, range(parts - 1, -1, -1))):
+        mine = mine.reshape(vision.shape)
+        for h in order:
+            over(h).wait_recv()
+            other = jnp.where(me_seq > 0, passed[1, h].astype(jnp.float32), 0.0)
+            vision[h] = (mine[h] + other).astype(jnp.bfloat16)
+            cast(h, h, 0).start()
+            cast(h, parts + h, 2).start()
+        for h in order:
+            over(h).wait_send()
+            cast(h, h, 0).wait_send()
+            cast(h, parts + h, 2).wait_send()
+
+    for me, mine in handed.items():
         @pl.when(section == me)
         def _():
-            for h in list(order)[: parts // 2]:
+            for h in order:
                 cast(h, h, 1).wait_recv()
-                cast(h, h, 1).start()
-            for h in list(order)[parts // 2 :]:
-                cast(h, h, 1).wait_recv()
-            for h in list(order)[: parts // 2]:
+                if h in mine:
+                    cast(h, h, 1).start()
+            for h in mine:
                 cast(h, h, 1).wait_send()
 
     @pl.when(section == 1)
@@ -506,10 +520,11 @@
             pltpu.VMEM(patches.shape, bf), pltpu.VMEM(text.shape, bf), *spread,
             big, big, pltpu.VMEM((NC, NZ, rows, 128), bf), big, big,
             pltpu.VMEM((CHUNKS, CHUNK, width), bf), pltpu.VMEM((CHUNKS, CHUNK, width), bf),
-            pltpu.VMEM((2, text.shape[0], width), bf), pltpu.VMEM((4, text.shape[0] // 4, width), bf),
+            pltpu.VMEM((2, 4, text.shape[0] // 4, width), bf), pltpu.VMEM((4, text.shape[0] // 4, width), bf),
             pltpu.SemaphoreType.DMA((ENC_COPIES,)), pltpu.SemaphoreType.DMA((ENC_COPIES,)),
-            pltpu.SemaphoreType.DMA((CHUNKS,)), pltpu.SemaphoreType.DMA((CHUNKS,)),
+            pltpu.SemaphoreType.DMA((CHUNKS, pl.cdiv(width, WIDTH))), pltpu.SemaphoreType.DMA((CHUNKS, pl.cdiv(width, WIDTH))),
             pltpu.SemaphoreType.DMA((8,)), pltpu.SemaphoreType.DMA((4,)),
+            pltpu.SemaphoreType.DMA((4,)), pltpu.SemaphoreType.DMA((4,)),
             pltpu.SemaphoreType.DMA((16,)),
         ],
         compiler_params=pltpu.CompilerParams(collective_id=0, has_side_effects=True, vmem_limit_bytes=60 << 20),
@@ -553,7 +568,7 @@
     queries, stacked = encode(
         frame_start, frame_count, fc_in[0], fc_out[0].T, proj_weight, patches[0],
         fc_gain, fc_in_bias, fc_out_bias, text_embed,
-        norm_gain[None], query_weight, key_weight, value_weight, query_bias[None], value_bias[None],
+        norm_gain, query_weight, key_weight, value_weight, query_bias[None], value_bias[None],
         jnp.concatenate([cosine, cosine], axis=1), jnp.concatenate([-sine, sine], axis=1),
     )
     attended = attend(queries, stacked, segment_ids, shard_id, shard_rows)

time: 180 us -> 173 us (0.961)
  Pallas kernels: 173 us -> 168 us
    pallas_call x1, Pallas kernels: 135 us -> 131 us  [encode(): pl.pallas_call(encoder_kernel, out_shape=(jax.ShapeDtypeStruct((text.shap...]
where the time goes in v4:
time: 173 us
  Pallas kernels  168 us (97%)
  local copies, waits for them, and re-layouts  4.3 us (2%)
    pallas_call x1, Pallas kernels, encode(): pl.pallas_call(encoder_kernel, out_shape=(jax.ShapeDtypeStruct((text.shap...  131 us
    pallas_call x1, Pallas kernels, attend(): pl.pallas_call(attend_kernel, out_shape=jax.ShapeDtypeStruct(q.shape, jnp...  37.1 us

profile of v4, /device:TPU:232, one launch (start us, length us, event | category | flops | bytes accessed | tf_op | source)
XLA Modules:
  0.0 173.1 jit_solution(4114318250468889022)
XLA Ops:
  0.0 0.8 dynamic_slice.3
  0.8 0.9 reshape.23
  1.7 0.1 reshape.24.kseg_ref
  1.8 0.3 fusion
  2.1 0.8 pad_maximum_fusion
  2.9 130.6 %encode.1 = (bf16[512,128]{1,0:T(8,128)(2,1)}, bf16[128,256]{1,0:T(8,128)(2,1)}) custom-call(s32[64]{0:T(128)} %start_ref.1, s32[64]{0:T(128)} %count_ref.1, bf16[18,2176]{1,0:T(8,128)(2,1)} %bitcast.20, bf16[18,2176]{1,0:T(8,128)(2,1)} %bitcast.21, bf16[18,3584]{1,0:T(8,128)(2,1)} %proj_ref.1, bf16[729,1152]{1,0:T(8,128)(2,1)} %bitcast.19, ...), custom_call_target="tpu_custom_call" | custom-call | flops 10000000000 | bytes 40000000 | tf_op jit(solution)/shard_map/encode/pallas_call | solution.py:508
  133.4 0.1 copy.20.qseg_ref
  133.6 0.0 copy-start
  133.6 0.9 copy-done
  134.5 0.0 copy-start.1
  134.5 0.8 copy-done.1
  135.3 37.1 %attend.1 = bf16[512,128]{1,0:T(8,128)(2,1)S(1)} custom-call(bf16[128,256]{1,0:T(8,128)(2,1)S(1)} %copy-done.1, bf16[512,128]{1,0:T(8,128)(2,1)S(1)} %copy-done, s32[512,1]{1,0:T(8,128)S(1)} %copy.20.qseg_ref, s32[8,2,2,256]{3,2,1,0:T(2,128)S(1)} %reshape.24.kseg_ref), custom_call_target="tpu_custom_call" | custom-call | flops 2000000000 | bytes 40000000 | tf_op jit(solution)/shard_map/attend/pallas_call | solution.py:190
  172.4 0.7 copy.24
  (4 shorter events, 0.0 us)
Async XLA Ops:
  133.6 0.9 copy-start
  134.5 0.8 copy-start.1

commit v5 on v4

--- a/solution.py
+++ b/solution.py
@@ -41,7 +41,7 @@
     for t in targets:
         t = {"seq": t} if not isinstance(t, dict) else t
         pl.semaphore_signal(barrier, inc=1, device_id=t, device_id_type=pl.DeviceIdType.MESH)
-    pl.semaphore_wait(barrier, len(targets))
+    return lambda: pl.semaphore_wait(barrier, len(targets))
 
 
 def torus_gather(ring, me, a_one, a_many, b_one, b_many, b_like_a=False):
@@ -101,6 +101,7 @@
 ):
     me_seq = lax.axis_index("seq")
     z, x, c = me_seq // (NX * NC), lax.rem(me_seq // NC, NX), lax.rem(me_seq, NC)
+    greeted = greet([seq_id(z + 1, x, c), seq_id(z - 1, x, c), seq_id(z, x + 1, c), seq_id(z, x - 1, c), seq_id(z, x, 1 - c)])
     half = kv_ref.shape[0] // 2
     mine = [
         pltpu.make_async_copy(kv_ref.at[pl.ds(0, half)], a_ref.at[z, x, c], own_sem.at[0]),
@@ -110,7 +111,7 @@
         copy.start()
     queries = pltpu.make_async_copy(q_hbm, q_ref, own_sem.at[2])
     queries.start()
-    greet([seq_id(z + 1, x, c), seq_id(z - 1, x, c), seq_id(z, x + 1, c), seq_id(z, x - 1, c), seq_id(z, x, 1 - c)])
+    greeted()
     for copy in mine:
         copy.wait()
     ring = Ring(send_sem, recv_sem)
@@ -205,9 +206,9 @@
     )(kv, q, qseg, kseg)
 
 
-CHUNKS, CHUNK = 8, 96
+CHUNKS, CHUNK, LAST = 8, 96, 64
 HEAD_START, EVERY = 2, 2
-WIDTH = 1152
+WIDTH = 256
 SPLIT = 112
 ENC_COPIES = 14 + 2 * (3 * 31 + 12) + 8
 layer_eps = 1e-06
@@ -234,6 +235,10 @@
     sources = [lax.rem(j + 8 - k, 8) for k in range(8)]
     member = lambda k: z * (NX * NC) + k
 
+    greeted = greet(
+        [member(k) for k in others[1:]]
+        + [seq_id(z + 1, x, c), seq_id(z - 1, x, c), ahead, behind, {"section": up}, {"section": down}]
+    )
     frame = pltpu.make_async_copy(patches_ref, frame_ref, local_sem.at[2])
     text = pltpu.make_async_copy(text_hbm, text_ref, local_sem.at[11])
     heads = qw_hbm.shape[1]
@@ -249,6 +254,7 @@
     def _():
         frame.start()
 
+    inflow[CHUNKS - 1, LAST:] = jnp.zeros((CHUNK - LAST, inflow.shape[2]), inflow.dtype)
     depth = in_ref.shape[0]
     w_ref[:, 16:, :] = jnp.zeros((8, 16, w_ref.shape[2]), w_ref.dtype)
     p_ref[:, 16:, :] = jnp.zeros((8, 16, p_ref.shape[2]), p_ref.dtype)
@@ -269,10 +275,7 @@
     inner = slot & 31
     pick = jnp.where((inner < depth) & (at == depth * (slot >> 5) + inner), 1.0, 0.0).astype(jnp.bfloat16)
 
-    greet(
-        [member(k) for k in others[1:]]
-        + [seq_id(z + 1, x, c), seq_id(z - 1, x, c), ahead, behind, {"section": up}, {"section": down}]
-    )
+    greeted()
     ring = Ring(send_sem, recv_sem)
     spread_w = [ring.copy(w_ref.at[others[k]], rec_w.at[sources[k]], member(others[k]), rec_w.at[j]) for k in range(1, 8)]
     spread_p = [ring.copy(p_ref.at[others[k]], rec_p.at[sources[k]], member(others[k]), rec_p.at[j]) for k in range(1, 8)]
@@ -361,20 +364,20 @@
         token = jnp.where((token >= 0) & (token < kept), token, -2)
         select_ref[...] = jnp.where(token == cell, share, 0.0).astype(jnp.bfloat16)
 
-    columns = [(at, min(WIDTH, 8 * rows - at)) for at in range(0, 8 * rows, WIDTH)]
-
-    def chunk_copy(i, n):
-        at, size = columns[n]
+    def chunk_copy(i, size):
         return pltpu.make_async_remote_copy(
-            src_ref=outflow.at[i, :, pl.ds(at, size)], dst_ref=inflow.at[i, :, pl.ds(at, size)],
-            send_sem=chunk_send.at[i, n], recv_sem=chunk_recv.at[i, n],
+            src_ref=outflow.at[i, pl.ds(0, size)], dst_ref=inflow.at[i, pl.ds(0, size)],
+            send_sem=chunk_send.at[i], recv_sem=chunk_recv.at[i],
             device_id={"section": up}, device_id_type=pl.DeviceIdType.MESH)
 
     def one_chunk(i, nothing):
-        @pl.when(section > 0)
+        @pl.when((section > 0) & (i < CHUNKS - 1))
         def _():
-            for n in range(len(columns)):
-                chunk_copy(i, n).wait_recv()
+            chunk_copy(i, CHUNK).wait_recv()
+
+        @pl.when((section > 0) & (i == CHUNKS - 1))
+        def _():
+            chunk_copy(i, LAST).wait_recv()
 
         widened = inflow[i].astype(jnp.float32)
         center = widened - jnp.mean(widened, axis=1, keepdims=True)
@@ -388,8 +391,8 @@
         flat = lambda ref, k: ref[k // 2, k % 2].reshape(8 * rows, 256)
         parts = [hidden(flat(win, k), bin_ref[:, 256 * k : 256 * k + 256]) for k in range(8)]
         parts.append(hidden(extra[0].reshape(8 * rows, 128), bin_ref[:, 2048:]))
-        for n, (at, size) in enumerate(columns):
-            to = at + size
+        for at in range(0, 8 * rows, WIDTH):
+            to = min(at + WIDTH, 8 * rows)
             out = widened[:, at:to] + bout_ref[:, at:to]
             for k in range(9):
                 w_out = flat(wout, k) if k < 8 else extra[1].reshape(8 * rows, 128)
@@ -397,9 +400,13 @@
                     parts[k], w_out[at:to], (((1,), (1,)), ((), ())), preferred_element_type=jnp.float32)
             outflow[i, :, at:to] = out.astype(jnp.bfloat16)
 
-            @pl.when(jnp.logical_not(last))
-            def _():
-                chunk_copy(i, n).start()
+        @pl.when(jnp.logical_not(last) & (i < CHUNKS - 1))
+        def _():
+            chunk_copy(i, CHUNK).start()
+
+        @pl.when(jnp.logical_not(last) & (i == CHUNKS - 1))
+        def _():
+            chunk_copy(i, LAST).start()
 
         for n, stage in enumerate(p_stages):
             @pl.when((i == EVERY * (n - HEAD_START * section)) & (section > 0))
@@ -418,8 +425,7 @@
     @pl.when(jnp.logical_not(last))
     def _():
         for i in range(CHUNKS):
-            for n in range(len(columns)):
-                chunk_copy(i, n).wait_send()
+            chunk_copy(i, CHUNK if i < CHUNKS - 1 else LAST).wait_send()
 
     over = lambda h: pltpu.make_async_remote_copy(
         src_ref=passed.at[0, h], dst_ref=passed.at[1, h], send_sem=over_send.at[h], recv_sem=over_recv.at[h],
@@ -522,7 +528,7 @@
             pltpu.VMEM((CHUNKS, CHUNK, width), bf), pltpu.VMEM((CHUNKS, CHUNK, width), bf),
             pltpu.VMEM((2, 4, text.shape[0] // 4, width), bf), pltpu.VMEM((4, text.shape[0] // 4, width), bf),
             pltpu.SemaphoreType.DMA((ENC_COPIES,)), pltpu.SemaphoreType.DMA((ENC_COPIES,)),
-            pltpu.SemaphoreType.DMA((CHUNKS, pl.cdiv(width, WIDTH))), pltpu.SemaphoreType.DMA((CHUNKS, pl.cdiv(width, WIDTH))),
+            pltpu.SemaphoreType.DMA((CHUNKS,)), pltpu.SemaphoreType.DMA((CHUNKS,)),
             pltpu.SemaphoreType.DMA((8,)), pltpu.SemaphoreType.DMA((4,)),
             pltpu.SemaphoreType.DMA((4,)), pltpu.SemaphoreType.DMA((4,)),
             pltpu.SemaphoreType.DMA((16,)),

time: 173 us -> 172 us (level)
  Pallas kernels: 168 us -> 166 us
    pallas_call x1, Pallas kernels: 131 us -> 129 us  [encode(): pl.pallas_call(encoder_kernel, out_shape=(jax.ShapeDtypeStruct((text.shap...]
where the time goes in v5:
time: 172 us
  Pallas kernels  166 us (97%)
  local copies, waits for them, and re-layouts  4.3 us (2%)
    pallas_call x1, Pallas kernels, encode(): pl.pallas_call(encoder_kernel, out_shape=(jax.ShapeDtypeStruct((text.shap...  129 us
    pallas_call x1, Pallas kernels, attend(): pl.pallas_call(attend_kernel, out_shape=jax.ShapeDtypeStruct(q.shape, jnp...  37.6 us

profile of v5, /device:TPU:232, one launch (start us, length us, event | category | flops | bytes accessed | tf_op | source)
XLA Modules:
  0.0 171.6 jit_solution(15231353603894251116)
XLA Ops:
  0.0 0.8 dynamic_slice.3
  0.8 0.9 reshape.23
  1.7 0.1 reshape.24.kseg_ref
  1.8 0.3 fusion
  2.1 0.8 pad_maximum_fusion
  2.9 128.5 %encode.1 = (bf16[512,128]{1,0:T(8,128)(2,1)}, bf16[128,256]{1,0:T(8,128)(2,1)}) custom-call(s32[64]{0:T(128)} %start_ref.1, s32[64]{0:T(128)} %count_ref.1, bf16[18,2176]{1,0:T(8,128)(2,1)} %bitcast.20, bf16[18,2176]{1,0:T(8,128)(2,1)} %bitcast.21, bf16[18,3584]{1,0:T(8,128)(2,1)} %proj_ref.1, bf16[729,1152]{1,0:T(8,128)(2,1)} %bitcast.19, ...), custom_call_target="tpu_custom_call" | custom-call | flops 10000000000 | bytes 40000000 | tf_op jit(solution)/shard_map/encode/pallas_call | solution.py:514
  131.4 0.1 copy.20.qseg_ref
  131.6 0.0 copy-start
  131.6 0.9 copy-done
  132.5 0.0 copy-start.1
  132.5 0.8 copy-done.1
  133.3 37.6 %attend.1 = bf16[512,128]{1,0:T(8,128)(2,1)S(1)} custom-call(bf16[128,256]{1,0:T(8,128)(2,1)S(1)} %copy-done.1, bf16[512,128]{1,0:T(8,128)(2,1)S(1)} %copy-done, s32[512,1]{1,0:T(8,128)S(1)} %copy.20.qseg_ref, s32[8,2,2,256]{3,2,1,0:T(2,128)S(1)} %reshape.24.kseg_ref), custom_call_target="tpu_custom_call" | custom-call | flops 2000000000 | bytes 40000000 | tf_op jit(solution)/shard_map/attend/pallas_call | solution.py:191
  170.9 0.7 copy.24
  (4 shorter events, 0.0 us)
Async XLA Ops:
  131.6 0.9 copy-start
  132.5 0.8 copy-start.1
